TPU v7x, 256 devices: a whole 4x4x8 slice. The times are simulated.
256 devices in a mesh: bank: 64 (over z, y, core), zero: 4 (over x).
Axes of the slice: x: 4, y: 4, z: 8, core: 2. Of those that a mesh axis runs over, the one named last changes fastest.
Arguments:
- w_gate: float32 [64, 2048, 1024], P('bank', 'zero'), may hold values from -0.1875 to 0.1875
- avg_gate: float32 [64, 2048, 1024], P('bank', 'zero'), may hold values from -0.125 to 0.125
- w_up: float32 [64, 2048, 1024], P('bank', 'zero'), may hold values from -0.1875 to 0.1875
- avg_up: float32 [64, 2048, 1024], P('bank', 'zero'), may hold values from -0.125 to 0.125
- mix_share: float32 [64], P('bank'), may hold values from 0.2 to 0.8
- router_weight: float32 [2048, 64], P('zero', 'bank'), may hold values from -0.125 to 0.125
- router_gain: float32 [2048], P('zero'), may hold values from 0.25 to 1.75
Outputs:
- serve_gate: bfloat16 [64, 2048, 1024], P('bank')
- serve_up: bfloat16 [64, 2048, 1024], P('bank')
- scale_gate: float32 [64, 1024], P('bank')
- scale_up: float32 [64, 1024], P('bank')
- serve_router: bfloat16 [2048, 64], replicated
All inputs are finite; a program needn't handle non-finite values.
Results may differ from a plain program's by a relative error of at most 0.001.
Values may be sent and summed in bfloat16 or wider, within the bound.
A program may use at most 64 MiB of HBM per device.

v0:
```python
import jax
import jax.numpy as jnp
from jax import lax
from jax.sharding import PartitionSpec as P


def copy_for_each(x, axis):
    peers = lax.axis_size(axis)
    return lax.all_to_all(jnp.broadcast_to(x[None], (peers, *x.shape)), axis, 0, 0, tiled=True)


def taken_together(x, axis):
    everything = copy_for_each(x, axis)
    return jnp.sum(everything, axis=0)


def together(arrays, axis):
    vector, at, done = (jnp.concatenate([a.reshape(-1) for a in arrays]), 0, [])
    so_far = taken_together(vector, axis)
    for a in arrays:
        done.append(so_far[at : at + a.size].reshape(a.shape))
        at += a.size
    return tuple(done)


def in_one_piece(arrays, axis, dim, along):
    both = jnp.concatenate(arrays, axis=along)
    out, at, done = (lax.all_gather(both, axis, axis=dim, tiled=True), 0, [])
    for a in arrays:
        done.append(lax.slice_in_dim(out, at, at + a.shape[along], axis=along))
        at += a.shape[along]
    return tuple(done)


def in_order(blocks, dim):
    dims = list(blocks.shape[1:])
    dims[dim] *= blocks.shape[0]
    return jnp.moveaxis(blocks, 0, dim).reshape(dims)


def collect(x, axis, dim):
    return in_order(copy_for_each(x, axis), dim)


def local(w_gate, avg_gate, w_up, avg_up, mix_share, router_weight, router_gain):
    fresh_gate = mix_share[:, None, None] * w_gate + (1.0 - mix_share[:, None, None]) * avg_gate
    fresh_up = mix_share[:, None, None] * w_up + (1.0 - mix_share[:, None, None]) * avg_up
    total_gate, total_up = together(
        (jnp.sum(fresh_gate * fresh_gate, axis=1), jnp.sum(fresh_up * fresh_up, axis=1)), "zero"
    )
    scale_gate = jnp.sqrt(total_gate)
    scale_up = jnp.sqrt(total_up)
    narrow_gate, narrow_up = (
        (fresh_gate / jnp.expand_dims(scale_gate, 1)).astype(jnp.bfloat16),
        (fresh_up / jnp.expand_dims(scale_up, 1)).astype(jnp.bfloat16),
    )
    serve_gate, serve_up = in_one_piece((narrow_gate, narrow_up), "zero", 1, 0)
    part_router = (router_weight * router_gain[:, None]).astype(jnp.bfloat16)
    row_router = lax.all_gather(part_router, "zero", axis=0, tiled=True)
    serve_router = collect(row_router, "bank", 1)
    return (serve_gate, serve_up, scale_gate, scale_up, serve_router)


def solution(mesh):
    placed = (
        P("bank", "zero", None),
        P("bank", "zero", None),
        P("bank", "zero", None),
        P("bank", "zero", None),
        P("bank"),
        P("zero", "bank"),
        P("zero"),
    )
    return jax.shard_map(
        local,
        mesh=mesh,
        in_specs=placed,
        out_specs=(
            P("bank", None, None),
            P("bank", None, None),
            P("bank", None),
            P("bank", None),
            P(),
        ),
        check_vma=False,
    )
```

profile of v0, /device:TPU:8, one launch (start us, length us, event | category | flops | bytes accessed | tf_op | source)
XLA Modules:
  0.0 126.7 jit_solution(15111544975916829221)
XLA Ops:
  7.2 0.0 all-gather.2.cloned.1.call-start
  7.9 0.0 copy-start
  7.9 0.0 copy-start.1
  7.9 2.8 %multiply_reduce_fusion.1 = f32[1024]{0:T(1024)S(1)} fusion(f32[1,512,1024]{2,1,0:T(8,128)} %param.8, f32[]{:T(128)} %bitcast.1, f32[1,512,1024]{2,1,0:T(8,128)} %param.7, f32[]{:T(128)} %bitcast.13), kind=kLoop, calls=%fused_computation.5 | loop fusion | flops 2620416 | bytes 4198408 | tf_op jit(solution)/shard_map/reduce_sum | solution.py:49
  10.7 0.1 copy-done
  10.7 0.6 copy-done.1
  11.3 0.5 multiply_reduce_fusion
  11.9 9.5 %all_to_all.11 = f32[4,1,2048]{2,1,0:T(1,128)S(1)} all-to-all(f32[4,1,2048]{2,1,0:T(1,128)S(1)} %broadcast_in_dim.8), channel_id=1, replica_groups=mesh['bank'=64,'zero'=4] {'zero'}, dimensions={0} | all-to-all | bytes 65536 | tf_op jit(solution)/shard_map/all_to_all | solution.py:9
  21.5 0.0 copy-start.2
  21.5 0.0 copy-start.3
  21.5 4.0 %divide_convert_fusion = (bf16[1,512,1024]{2,1,0:T(8,128)(2,1)S(1)}, bf16[1,512,1024]{2,1,0:T(8,128)(2,1)S(1)}) fusion(f32[1024]{0:T(1024)S(1)} %get-tuple-element.8, f32[1,512,1024]{2,1,0:T(8,128)S(1)} %copy-done, f32[]{:T(128)} %bitcast.1, f32[1,512,1024]{2,1,0:T(8,128)} %param.9, f32[]{:T(128)} %bitcast.15, f32[1024]{0:T(1024)S(1)} %get-tuple-element.7, ...), kind=kLoop, calls=%fused_computation.1 | loop fusion | flops 5242880 | bytes 10493960 | tf_op jit(solution)/shard_map/convert_element_type | solution.py:55
  25.5 0.0 copy-done.2
  25.5 0.0 copy-done.3
  25.5 1.5 %pad_maximum_fusion = bf16[2,512,1024]{2,1,0:T(8,128)(2,1)} fusion(bf16[1,512,1024]{2,1,0:T(8,128)(2,1)S(1)} %get-tuple-element.9, bf16[1,512,1024]{2,1,0:T(8,128)(2,1)S(1)} %get-tuple-element.10), kind=kLoop, calls=%fused_computation | loop fusion | flops 1048576 | bytes 4194304 | tf_op jit(solution)/shard_map/concatenate | solution.py:27
  27.0 0.0 copy-start.4
  27.0 0.0 copy-start.5
  27.0 0.0 all-gather.2.cloned.1.call-update
  27.0 0.7 copy-done.4
  27.7 0.0 copy-done.5
  27.7 10.4 %all_gather.7 = bf16[2048,1]{0,1:T(2,128)(2,1)S(1)} all-gather(bf16[512,1]{0,1:T(2,128)(2,1)S(1)} %multiply_convert_fusion), channel_id=1, replica_groups=mesh['bank'=64,'zero'=4] {'zero'}, dimensions={0}, use_global_device_ids=true | all-gather | bytes 5120 | tf_op jit(solution)/shard_map/all_gather | solution.py:59
  38.2 0.3 broadcast_bitcast_fusion
  38.4 0.5 broadcast.11
  39.0 2.2 %reduce.4 = bf16[64,2048]{1,0:T(8,128)(2,1)S(1)} reduce(bf16[64,1,2048]{2,1,0:T(2,128)(2,1)S(1)} %broadcast_bitcast_fusion, bf16[]{:T(256)} %broadcast.11), dimensions={1}, to_apply=%broadcast_bitcast_fusion.reduce_sub_computation | reduce | bytes 524290
  41.1 0.2 reshape.50
  41.3 24.1 %all_to_all.12 = bf16[64,2,1024]{2,1,0:T(2,128)(2,1)S(1)} all-to-all(bf16[64,2,1024]{2,1,0:T(2,128)(2,1)S(1)} %reshape.50), channel_id=1, replica_groups=mesh['bank'=64,'zero'=4] {'bank'}, dimensions={0} | all-to-all | bytes 524288 | tf_op jit(solution)/shard_map/all_to_all | solution.py:9
  65.4 0.2 reshape.51
  65.6 0.9 copy.20
  66.5 47.3 %all-gather.2.cloned.1.call-done = bf16[2,2048,1024]{2,1,0:T(8,128)(2,1)} async-done(((bf16[2,512,1024]{2,1,0:T(8,128)(2,1)}), bf16[2,2048,1024]{2,1,0:T(8,128)(2,1)}) %all-gather.2.cloned.1.call-update) | async-done | bytes 8388624 | tf_op jit(solution)/shard_map/all_gather | solution.py:28
  113.8 6.0 %fusion = (bf16[1,2048,1024]{2,1,0:T(8,128)(2,1)}, bf16[1,2048,1024]{2,1,0:T(8,128)(2,1)}) fusion(bf16[2,2048,1024]{2,1,0:T(8,128)(2,1)} %all-gather.2.cloned.1.call-done), kind=kLoop, calls=%fused_computation.12 | loop fusion | bytes 16777216 | tf_op jit(solution)/shard_map/slice | solution.py:30
  (6 shorter events, 0.1 us)
Async XLA Ops:
  7.2 106.6 %all-gather.2.cloned.1.call-start = ((), (), s32[]{:S(2)}) async-start(), calls=%async_computation.2 | async-start | bytes 10485760 | tf_op jit(solution)/shard_map/all_gather | solution.py:28
  7.9 2.9 %copy-start = (f32[1,512,1024]{2,1,0:T(8,128)S(1)}, f32[1,512,1024]{2,1,0:T(8,128)}, u32[]{:S(2)}) copy-start(f32[1,512,1024]{2,1,0:T(8,128)} %param.10) | copy-start | bytes 6291460
  7.9 3.5 %copy-start.1 = (f32[1,512,1024]{2,1,0:T(8,128)S(1)}, f32[1,512,1024]{2,1,0:T(8,128)}, u32[]{:S(2)}) copy-start(f32[1,512,1024]{2,1,0:T(8,128)} %param.9) | copy-start | bytes 6291460
  21.5 4.0 %copy-start.2 = (f32[1024]{0:T(1024)}, f32[1024]{0:T(1024)S(1)}, u32[]{:S(2)}) copy-start(f32[1024]{0:T(1024)S(1)} %get-tuple-element.7) | copy-start | bytes 12292
  21.5 4.0 %copy-start.3 = (f32[1024]{0:T(1024)}, f32[1024]{0:T(1024)S(1)}, u32[]{:S(2)}) copy-start(f32[1024]{0:T(1024)S(1)} %get-tuple-element.8) | copy-start | bytes 12292
  27.0 0.7 copy-start.4
  27.0 0.7 copy-start.5
Sparse Core Ops, SparseCore 0:
  27.1 86.6 all-gather.1
where the time goes:
time: 128 us; the launch traced here: 127 us
  waiting for transfers between devices  47.3 us (37%)
  blocking collectives  44.1 us (34%)
  between operations  14.8 us (12%)
  other arithmetic  11 us (9%)
  local copies, waits for them, and re-layouts  9.47 us (7%)
    all_gather x1, waiting for transfers between devices, in_one_piece(): out, at, done = (lax.all_gather(both, axis, axis=dim, tiled=True), 0, [])  47.3 us
    all_to_all x2, blocking collectives, copy_for_each(): lax.all_to_all(jnp.broadcast_to(x[None], (peers, *x.shape)), axis, 0, 0,...  33.6 us
    all_gather x1, blocking collectives, local(): row_router = lax.all_gather(part_router, 'zero', axis=0, tiled=True)  10.4 us
    slice x1, local copies, waits for them, and re-layouts, in_one_piece(): done.append(lax.slice_in_dim(out, at, at + a.shape[along], axis=along))  6.02 us
    convert_element_type x1, other arithmetic, local(): (fresh_up / jnp.expand_dims(scale_up, 1)).astype(jnp.bfloat16)  3.95 us
    reduce_sum x1, other arithmetic, local(): jnp.sum(fresh_gate * fresh_gate, axis=1)  2.78 us
    unnamed x16, local copies, waits for them, and re-layouts  2.57 us
  transfers between devices with their start and end apart: 1, of which 1 were waited for; matrix products, arithmetic and copies ran while one was open for 3% of the time, Pallas kernels for 0%

commit v1 on v0

v1 whole, which is shorter than its diff:
```python
import jax
import jax.numpy as jnp
from jax import lax
from jax.experimental import pallas as pl
from jax.experimental.pallas import tpu as pltpu
from jax.sharding import PartitionSpec as P

MESH = pl.DeviceIdType.MESH
ROWS = 512
COLS = 1024
WIDTH = 256
PER = COLS // WIDTH
CHUNKS = 2 * PER
STEP = 64
RB = 16


def kernel(
    w_gate, avg_gate, w_up, avg_up, mix, router_w, router_g,
    o_gate, o_up, o_sgate, o_sup, o_router,
    wide, other, wide_sem, other_sem, mix_s, mix_sem, rw, rg, rw_sem, rg_sem,
    sums0, sums1, scale, sums_send, sums_recv,
    narrow, send_r, send_l, recv_l, recv_r, fsend, frecv, put, put_far,
    xr, bank_r, out_r, rx_send, rx_recv, rc, ry, rz, small,
):
    bank = lax.axis_index("bank")
    me = lax.axis_index("zero")
    right, left, across = lax.rem(me + 1, 4), lax.rem(me + 3, 4), lax.rem(me + 2, 4)
    core = lax.rem(bank, 2)
    yy = lax.rem(bank // 2, 4)
    zz = bank // 8

    def at_bank(z, y, c):
        return (z * 4 + y) * 2 + c

    twin = at_bank(zz, yy, 1 - core)
    y_up, y_down = at_bank(zz, lax.rem(yy + 1, 4), core), at_bank(zz, lax.rem(yy + 3, 4), core)
    z_up, z_down = at_bank(lax.rem(zz + 1, 8), yy, core), at_bank(lax.rem(zz + 7, 8), yy, core)

    w_in, a_in = (w_gate, w_up), (avg_gate, avg_up)

    mix_copy = pltpu.make_async_copy(mix, mix_s, mix_sem)
    mix_copy.start()
    loads = []
    for c in range(CHUNKS):
        m, cols = c // PER, pl.ds((c % PER) * WIDTH, WIDTH)
        first = pltpu.make_async_copy(w_in[m].at[:, cols], wide.at[c], wide_sem.at[c])
        second = pltpu.make_async_copy(a_in[m].at[:, cols], other.at[c], other_sem.at[c])
        first.start()
        second.start()
        loads.append((first, second))
    load_rw = pltpu.make_async_copy(router_w, rw, rw_sem)
    load_rg = pltpu.make_async_copy(router_g, rg, rg_sem)
    load_rw.start()
    load_rg.start()

    barrier = pltpu.get_barrier_semaphore()
    for where in (
        (bank, right), (bank, left), (bank, across),
        (twin, me), (y_up, me), (y_down, me), (z_up, me), (z_down, me),
    ):
        pl.semaphore_signal(barrier, inc=1, device_id=where, device_id_type=MESH)

    mix_copy.wait()
    share = mix_s[0]
    rest = 1.0 - share

    def mixed(c):
        loads[c][0].wait()
        loads[c][1].wait()

        def step(i, acc):
            rows = pl.ds(i * STEP, STEP)
            fresh = share * wide[c, rows, :] + rest * other[c, rows, :]
            wide[c, rows, :] = fresh
            return acc + jnp.sum((fresh * fresh).reshape(STEP // 8, 8, WIDTH), axis=0)

        acc = lax.fori_loop(0, ROWS // STEP, step, jnp.zeros((8, WIDTH), jnp.float32))
        return jnp.sum(acc, axis=0, keepdims=True)

    peers = (right, left, across)

    def share_sums(buf, g):
        copies = []
        for k, peer in enumerate(peers):
            copy = pltpu.make_async_remote_copy(
                src_ref=buf.at[me], dst_ref=buf.at[me],
                send_sem=sums_send.at[g, k], recv_sem=sums_recv.at[g, k],
                device_id=(bank, peer), device_id_type=MESH,
            )
            copy.start()
            copies.append(copy)
        return copies

    sums0[me] = mixed(0)
    pl.semaphore_wait(barrier, 8)
    sent0 = share_sums(sums0, 0)

    load_rw.wait()
    load_rg.wait()
    prod = rw[...] * rg[...]
    for k in range(4):
        xr[me, pl.ds(k, 1), :] = prod[:, k * 128 : (k + 1) * 128]
    sent_x = []
    for k, peer in enumerate(peers):
        copy = pltpu.make_async_remote_copy(
            src_ref=xr.at[me], dst_ref=xr.at[me],
            send_sem=rx_send.at[k], recv_sem=rx_recv.at[k],
            device_id=(bank, peer), device_id_type=MESH,
        )
        copy.start()
        sent_x.append(copy)

    for c in range(1, CHUNKS):
        sums1[me, :, pl.ds((c - 1) * WIDTH, WIDTH)] = mixed(c)
    sent1 = share_sums(sums1, 1)

    def where_at(c, owner):
        return narrow.at[c // PER, pl.ds(owner * ROWS, ROWS), pl.ds((c % PER) * WIDTH, WIDTH)]

    def out_at(c, owner):
        return (o_gate, o_up)[c // PER].at[pl.ds(owner * ROWS, ROWS), pl.ds((c % PER) * WIDTH, WIDTH)]

    def write(c, owner, sem):
        copy = pltpu.make_async_copy(where_at(c, owner), out_at(c, owner), sem)
        copy.start()
        writes.append(copy)

    writes = []
    sent = []

    def normalised(c):
        s = scale[c // PER, :, pl.ds((c % PER) * WIDTH, WIDTH)]
        inverse = 1.0 / s

        def step(i, carry):
            rows = pl.ds(i * STEP, STEP)
            narrow[
                c // PER, pl.ds(pl.multiple_of(me * ROWS + i * STEP, STEP), STEP),
                pl.ds((c % PER) * WIDTH, WIDTH),
            ] = (wide[c, rows, :] * inverse).astype(jnp.bfloat16)
            return carry

        lax.fori_loop(0, ROWS // STEP, step, 0)
        for dest, send, recv in ((right, send_r, recv_l), (left, send_l, recv_r)):
            copy = pltpu.make_async_remote_copy(
                src_ref=where_at(c, me), dst_ref=where_at(c, me),
                send_sem=send.at[c], recv_sem=recv.at[c],
                device_id=(bank, dest), device_id_type=MESH,
            )
            copy.start()
            sent.append(copy)

    for copy in sent0:
        copy.wait_recv()
    scale[0, :, pl.ds(0, WIDTH)] = jnp.sqrt(((sums0[0] + sums0[1]) + sums0[2]) + sums0[3])
    normalised(0)
    for copy in sent1:
        copy.wait_recv()
    total = jnp.sqrt(((sums1[0] + sums1[1]) + sums1[2]) + sums1[3])
    scale[0, :, pl.ds(WIDTH, COLS - WIDTH)] = total[:, : COLS - WIDTH]
    scale[1, :, :] = total[:, COLS - WIDTH :]
    for c in range(1, CHUNKS):
        normalised(c)
    for c in range(CHUNKS):
        write(c, me, put.at[0, c])
    for m, o in enumerate((o_sgate, o_sup)):
        copy = pltpu.make_async_copy(scale.at[m], o, small.at[m])
        copy.start()
        writes.append(copy)

    for copy in sent_x:
        copy.wait_recv()
    for k in range(4):
        bank_r[bank, pl.ds(4 * k, 4), :] = xr[k]

    def push(first, count, dest, sems, k):
        block = bank_r.at[pl.ds(first, count)]
        copy = pltpu.make_async_remote_copy(
            src_ref=block, dst_ref=block, send_sem=sems.at[0, k], recv_sem=sems.at[1, k],
            device_id=(dest, me), device_id_type=MESH,
        )
        copy.start()
        sent.append(copy)
        return copy

    push(bank, 1, twin, rc, 0).wait_recv()
    pair = at_bank(zz, yy, 0)
    a = push(pair, 2, y_up, ry, 0)
    b = push(pair, 2, y_down, ry, 1)
    a.wait_recv()
    d = push(at_bank(zz, lax.rem(yy + 3, 4), 0), 2, y_up, ry, 2)
    b.wait_recv()
    d.wait_recv()
    ups = [push(zz * 8, 8, z_up, rz, 0)]
    downs = [push(zz * 8, 8, z_down, rz, 4)]
    for k in range(1, 4):
        ups[-1].wait_recv()
        ups.append(push(lax.rem(zz + 8 - k, 8) * 8, 8, z_up, rz, k))
        downs[-1].wait_recv()
        if k < 3:
            downs.append(push(lax.rem(zz + k, 8) * 8, 8, z_down, rz, 4 + k))
    ups[-1].wait_recv()
    for k in range(RB):
        out_r[:, k * 128 : (k + 1) * 128] = bank_r[:, k, :].astype(jnp.bfloat16)
    copy = pltpu.make_async_copy(out_r, o_router, small.at[2])
    copy.start()
    writes.append(copy)

    def forward(c, owner, dest):
        copy = pltpu.make_async_remote_copy(
            src_ref=where_at(c, owner), dst_ref=where_at(c, owner),
            send_sem=fsend.at[c], recv_sem=frecv.at[c],
            device_id=(bank, dest), device_id_type=MESH,
        )
        copy.start()
        return copy

    passed = []
    for c in range(CHUNKS):
        sent[2 * c].wait_recv()
        if c < PER:
            passed.append(forward(c, left, right))
        sent[2 * c + 1].wait_recv()
        if c >= PER:
            passed.append(forward(c, right, left))
        write(c, left, put.at[1, c])
        write(c, right, put.at[2, c])
    for c in range(PER):
        passed[c].wait_recv()
        write(c, across, put.at[3, c])
        passed[c + PER].wait_recv()
        write(c + PER, across, put.at[3, c + PER])

    for copy in sent0 + sent1 + sent_x + sent + passed:
        copy.wait_send()
    for copy in writes:
        copy.wait()


def local(w_gate, avg_gate, w_up, avg_up, mix_share, router_weight, router_gain):
    dma = pltpu.SemaphoreType.DMA
    f32, bf16 = jnp.float32, jnp.bfloat16
    anywhere = pl.BlockSpec(memory_space=pl.ANY)
    outs = pl.pallas_call(
        kernel,
        out_shape=(
            jax.ShapeDtypeStruct((4 * ROWS, COLS), bf16),
            jax.ShapeDtypeStruct((4 * ROWS, COLS), bf16),
            jax.ShapeDtypeStruct((1, COLS), f32),
            jax.ShapeDtypeStruct((1, COLS), f32),
            jax.ShapeDtypeStruct((64, RB * 128), bf16),
        ),
        in_specs=[anywhere] * 7,
        out_specs=[anywhere] * 5,
        scratch_shapes=[
            pltpu.VMEM((CHUNKS, ROWS, WIDTH), f32),
            pltpu.VMEM((CHUNKS, ROWS, WIDTH), f32),
            dma((CHUNKS,)),
            dma((CHUNKS,)),
            pltpu.SMEM((1,), f32),
            dma(()),
            pltpu.VMEM((1, ROWS), f32),
            pltpu.VMEM((1, ROWS), f32),
            dma(()),
            dma(()),
            pltpu.VMEM((4, 1, WIDTH), f32),
            pltpu.VMEM((4, 1, (CHUNKS - 1) * WIDTH), f32),
            pltpu.VMEM((2, 1, COLS), f32),
            dma((2, 3)),
            dma((2, 3)),
            pltpu.VMEM((2, 4 * ROWS, COLS), bf16),
            dma((CHUNKS,)),
            dma((CHUNKS,)),
            dma((CHUNKS,)),
            dma((CHUNKS,)),
            dma((CHUNKS,)),
            dma((CHUNKS,)),
            dma((4, CHUNKS)),
            dma((1,)),
            pltpu.VMEM((4, 4, 128), f32),
            pltpu.VMEM((64, RB, 128), f32),
            pltpu.VMEM((64, RB * 128), bf16),
            dma((3,)),
            dma((3,)),
            dma((2, 1)),
            dma((2, 3)),
            dma((2, 7)),
            dma((3,)),
        ],
        compiler_params=pltpu.CompilerParams(
            collective_id=0, has_side_effects=True, vmem_limit_bytes=67043328
        ),
        name="mean_and_gather",
    )(
        w_gate[0], avg_gate[0], w_up[0], avg_up[0], mix_share,
        router_weight.T, router_gain[None, :],
    )
    gate, up, sgate, sup, router = outs
    return gate[None], up[None], sgate, sup, router.T


def solution(mesh):
    placed = (
        P("bank", "zero", None),
        P("bank", "zero", None),
        P("bank", "zero", None),
        P("bank", "zero", None),
        P("bank"),
        P("zero", "bank"),
        P("zero"),
    )
    return jax.shard_map(
        local,
        mesh=mesh,
        in_specs=placed,
        out_specs=(
            P("bank", None, None),
            P("bank", None, None),
            P("bank", None),
            P("bank", None),
            P(),
        ),
        check_vma=False,
    )
```

time: 128 us -> 91.3 us (0.71)
  Pallas kernels: 0 us -> 81.1 us
  waiting for transfers between devices: 47.3 us -> 0 us
  blocking collectives: 44.1 us -> 0 us
  between operations: 14.8 us -> 1.3 us
  other arithmetic: 11 us -> 0 us
    pallas_call x0 -> x1, Pallas kernels: none -> 81.1 us  [local(): pl.pallas_call(kernel, out_shape=(jax.ShapeDtypeStruct((4 * ROWS, COLS),...]
    all_gather x1 -> x0, waiting for transfers between devices: 47.3 us -> none  [in_one_piece(): out, at, done = (lax.all_gather(both, axis, axis=dim, tiled=True), 0, [])]
    all_to_all x2 -> x0, blocking collectives: 33.6 us -> none  [copy_for_each(): lax.all_to_all(jnp.broadcast_to(x[None], (peers, *x.shape)), axis, 0, 0,...]
    all_gather x1 -> x0, blocking collectives: 10.4 us -> none  [local(): row_router = lax.all_gather(part_router, 'zero', axis=0, tiled=True)]
    unnamed x16 -> x13, local copies, waits for them, and re-layouts: 2.57 us -> 8.73 us
    slice x1 -> x0, local copies, waits for them, and re-layouts: 6.02 us -> none  [in_one_piece(): done.append(lax.slice_in_dim(out, at, at + a.shape[along], axis=along))]
    convert_element_type x2 -> x0, other arithmetic: 3.96 us -> none  [the longest x1 3.95 us: local(): (fresh_up / jnp.expand_dims(scale_up, 1)).astype(jnp.bfloat16)]
    reduce_sum x3 -> x0, other arithmetic: 3.32 us -> none  [the longest x1 2.78 us: local(): jnp.sum(fresh_gate * fresh_gate, axis=1)]
  transfers between devices with their start and end apart: 1 -> 0, of which waited for: 1 -> 0; matrix products, arithmetic and copies ran while one was open for 3% -> 0% of each run, Pallas kernels for 0% -> 0%
where the time goes in v1:
time: 91.3 us; the launch traced here: 91.2 us
  Pallas kernels  81.1 us (89%)
  local copies, waits for them, and re-layouts  8.73 us (10%)
  between operations  1.3 us (1%)
    pallas_call x1, Pallas kernels, local(): pl.pallas_call(kernel, out_shape=(jax.ShapeDtypeStruct((4 * ROWS, COLS),...  81.1 us
    unnamed x13, local copies, waits for them, and re-layouts  8.73 us

profile of v1, /device:TPU:8, one launch (start us, length us, event | category | flops | bytes accessed | tf_op | source)
XLA Modules:
  0.0 91.2 jit_solution(12531193168408621688)
XLA Ops:
  1.3 81.1 %mean_and_gather.1 = (bf16[2048,1024]{1,0:T(8,128)(2,1)}, bf16[2048,1024]{1,0:T(8,128)(2,1)}, f32[1,1024]{1,0:T(1,128)}, f32[1,1024]{1,0:T(1,128)}, bf16[64,2048]{1,0:T(8,128)(2,1)}) custom-call(f32[512,1024]{1,0:T(8,128)} %bitcast.11, f32[512,1024]{1,0:T(8,128)} %bitcast.12, f32[512,1024]{1,0:T(8,128)} %bitcast.13, f32[512,1024]{1,0:T(8,128)} %bitcast.14, ...), custom_call_target="tpu_custom_call" | custom-call | tf_op jit(solution)/shard_map/mean_and_gather/pallas_call | solution.py:245
  82.4 0.0 copy-start
  82.4 4.8 %copy.18 = bf16[1,2048,1024]{2,1,0:T(8,128)(2,1)} copy(bf16[1,2048,1024]{2,1,0:T(8,128)(2,1)} %bitcast.10) | data formatting | bytes 8388608
  87.2 0.0 copy-done
  87.3 0.0 copy-start.3
  87.3 0.0 copy-start.2
  87.3 0.0 copy-start.1
  87.3 2.0 %copy.19 = bf16[1,2048,1024]{2,1,0:T(8,128)(2,1)} copy(bf16[1,2048,1024]{2,1,0:T(8,128)(2,1)S(1)} %bitcast.9) | data formatting | bytes 8388608
  89.3 0.0 copy-done.3
  89.3 0.6 copy.20
  89.9 0.0 copy-done.2
  89.9 0.6 copy.21
  90.5 0.0 copy-done.1
  90.5 0.7 copy.22
Async XLA Ops:
  82.4 4.8 %copy-start = (bf16[2048,1024]{1,0:T(8,128)(2,1)S(1)}, bf16[2048,1024]{1,0:T(8,128)(2,1)}, u32[]{:S(2)}) copy-start(bf16[2048,1024]{1,0:T(8,128)(2,1)} %get-tuple-element.11) | copy-start | bytes 12582916
  87.3 2.0 %copy-start.3 = (f32[1,1024]{1,0:T(1,128)S(1)}, f32[1,1024]{1,0:T(1,128)}, u32[]{:S(2)}) copy-start(f32[1,1024]{1,0:T(1,128)} %get-tuple-element.22) | copy-start | bytes 12292
  87.3 2.6 %copy-start.2 = (f32[1,1024]{1,0:T(1,128)S(1)}, f32[1,1024]{1,0:T(1,128)}, u32[]{:S(2)}) copy-start(f32[1,1024]{1,0:T(1,128)} %get-tuple-element.23) | copy-start | bytes 12292
  87.3 3.2 %copy-start.1 = (bf16[64,2048]{1,0:T(8,128)(2,1)S(1)}, bf16[64,2048]{1,0:T(8,128)(2,1)}, u32[]{:S(2)}) copy-start(bf16[64,2048]{1,0:T(8,128)(2,1)} %get-tuple-element.14) | copy-start | bytes 786436

commit v2 on v1

--- a/solution.py
+++ b/solution.py
@@ -19,9 +19,9 @@
     w_gate, avg_gate, w_up, avg_up, mix, router_w, router_g,
     o_gate, o_up, o_sgate, o_sup, o_router,
     wide, other, wide_sem, other_sem, mix_s, mix_sem, rw, rg, rw_sem, rg_sem,
-    sums0, sums1, scale, sums_send, sums_recv,
-    narrow, send_r, send_l, recv_l, recv_r, fsend, frecv, put, put_far,
-    xr, bank_r, out_r, rx_send, rx_recv, rc, ry, rz, small,
+    sums0, sums1, sums_send, sums_recv,
+    send_r, send_l, recv_l, recv_r, fsend, frecv,
+    xr, bank_r, rx_send, rx_recv, rc, ry, rz,
 ):
     bank = lax.axis_index("bank")
     me = lax.axis_index("zero")
@@ -37,6 +37,7 @@
     y_up, y_down = at_bank(zz, lax.rem(yy + 1, 4), core), at_bank(zz, lax.rem(yy + 3, 4), core)
     z_up, z_down = at_bank(lax.rem(zz + 1, 8), yy, core), at_bank(lax.rem(zz + 7, 8), yy, core)
 
+    outs, scales = (o_gate, o_up), (o_sgate, o_sup)
     w_in, a_in = (w_gate, w_up), (avg_gate, avg_up)
 
     mix_copy = pltpu.make_async_copy(mix, mix_s, mix_sem)
@@ -62,7 +63,7 @@
         pl.semaphore_signal(barrier, inc=1, device_id=where, device_id_type=MESH)
 
     mix_copy.wait()
-    share = mix_s[0]
+    share = mix_s[...]
     rest = 1.0 - share
 
     def mixed(c):
@@ -116,27 +117,18 @@
     sent1 = share_sums(sums1, 1)
 
     def where_at(c, owner):
-        return narrow.at[c // PER, pl.ds(owner * ROWS, ROWS), pl.ds((c % PER) * WIDTH, WIDTH)]
-
-    def out_at(c, owner):
-        return (o_gate, o_up)[c // PER].at[pl.ds(owner * ROWS, ROWS), pl.ds((c % PER) * WIDTH, WIDTH)]
-
-    def write(c, owner, sem):
-        copy = pltpu.make_async_copy(where_at(c, owner), out_at(c, owner), sem)
-        copy.start()
-        writes.append(copy)
-
-    writes = []
+        return outs[c // PER].at[pl.ds(owner * ROWS, ROWS), pl.ds((c % PER) * WIDTH, WIDTH)]
+
     sent = []
 
     def normalised(c):
-        s = scale[c // PER, :, pl.ds((c % PER) * WIDTH, WIDTH)]
+        s = scales[c // PER][:, pl.ds((c % PER) * WIDTH, WIDTH)]
         inverse = 1.0 / s
 
         def step(i, carry):
             rows = pl.ds(i * STEP, STEP)
-            narrow[
-                c // PER, pl.ds(pl.multiple_of(me * ROWS + i * STEP, STEP), STEP),
+            outs[c // PER][
+                pl.ds(pl.multiple_of(me * ROWS + i * STEP, STEP), STEP),
                 pl.ds((c % PER) * WIDTH, WIDTH),
             ] = (wide[c, rows, :] * inverse).astype(jnp.bfloat16)
             return carry
@@ -153,21 +145,15 @@
 
     for copy in sent0:
         copy.wait_recv()
-    scale[0, :, pl.ds(0, WIDTH)] = jnp.sqrt(((sums0[0] + sums0[1]) + sums0[2]) + sums0[3])
+    o_sgate[:, pl.ds(0, WIDTH)] = jnp.sqrt(((sums0[0] + sums0[1]) + sums0[2]) + sums0[3])
     normalised(0)
     for copy in sent1:
         copy.wait_recv()
     total = jnp.sqrt(((sums1[0] + sums1[1]) + sums1[2]) + sums1[3])
-    scale[0, :, pl.ds(WIDTH, COLS - WIDTH)] = total[:, : COLS - WIDTH]
-    scale[1, :, :] = total[:, COLS - WIDTH :]
+    o_sgate[:, pl.ds(WIDTH, COLS - WIDTH)] = total[:, : COLS - WIDTH]
+    o_sup[...] = total[:, COLS - WIDTH :]
     for c in range(1, CHUNKS):
         normalised(c)
-    for c in range(CHUNKS):
-        write(c, me, put.at[0, c])
-    for m, o in enumerate((o_sgate, o_sup)):
-        copy = pltpu.make_async_copy(scale.at[m], o, small.at[m])
-        copy.start()
-        writes.append(copy)
 
     for copy in sent_x:
         copy.wait_recv()
@@ -202,10 +188,7 @@
             downs.append(push(lax.rem(zz + k, 8) * 8, 8, z_down, rz, 4 + k))
     ups[-1].wait_recv()
     for k in range(RB):
-        out_r[:, k * 128 : (k + 1) * 128] = bank_r[:, k, :].astype(jnp.bfloat16)
-    copy = pltpu.make_async_copy(out_r, o_router, small.at[2])
-    copy.start()
-    writes.append(copy)
+        o_router[:, k * 128 : (k + 1) * 128] = bank_r[:, k, :].astype(jnp.bfloat16)
 
     def forward(c, owner, dest):
         copy = pltpu.make_async_remote_copy(
@@ -224,17 +207,26 @@
         sent[2 * c + 1].wait_recv()
         if c >= PER:
             passed.append(forward(c, right, left))
-        write(c, left, put.at[1, c])
-        write(c, right, put.at[2, c])
     for c in range(PER):
         passed[c].wait_recv()
-        write(c, across, put.at[3, c])
         passed[c + PER].wait_recv()
-        write(c + PER, across, put.at[3, c + PER])
 
     for copy in sent0 + sent1 + sent_x + sent + passed:
         copy.wait_send()
-    for copy in writes:
+
+
+def put_out(gate, up, sgate, sup, router, o_gate, o_up, o_sgate, o_sup, o_router, sem):
+    copies = []
+    for i, (a, b) in enumerate(((gate, o_gate), (up, o_up))):
+        for k in range(4):
+            rows = pl.ds(k * ROWS, ROWS)
+            copies.append(pltpu.make_async_copy(a.at[rows], b.at[rows], sem.at[4 * i + k]))
+    copies.append(pltpu.make_async_copy(router, o_router, sem.at[8]))
+    copies.append(pltpu.make_async_copy(sgate, o_sgate, sem.at[9]))
+    copies.append(pltpu.make_async_copy(sup, o_sup, sem.at[10]))
+    for copy in copies:
+        copy.start()
+    for copy in copies:
         copy.wait()
 
 
@@ -242,23 +234,31 @@
     dma = pltpu.SemaphoreType.DMA
     f32, bf16 = jnp.float32, jnp.bfloat16
     anywhere = pl.BlockSpec(memory_space=pl.ANY)
-    outs = pl.pallas_call(
-        kernel,
-        out_shape=(
+    shapes = (
             jax.ShapeDtypeStruct((4 * ROWS, COLS), bf16),
             jax.ShapeDtypeStruct((4 * ROWS, COLS), bf16),
             jax.ShapeDtypeStruct((1, COLS), f32),
             jax.ShapeDtypeStruct((1, COLS), f32),
             jax.ShapeDtypeStruct((64, RB * 128), bf16),
-        ),
+    )
+    held = (
+            pltpu.VMEM((4 * ROWS, COLS), bf16),
+            pltpu.VMEM((4 * ROWS, COLS), bf16),
+            pltpu.VMEM((1, COLS), f32),
+            pltpu.VMEM((1, COLS), f32),
+            pltpu.VMEM((64, RB * 128), bf16),
+    )
+    outs = pl.pallas_call(
+        kernel,
+        out_shape=held,
         in_specs=[anywhere] * 7,
-        out_specs=[anywhere] * 5,
+        out_specs=[pl.BlockSpec(memory_space=pltpu.VMEM)] * 5,
         scratch_shapes=[
             pltpu.VMEM((CHUNKS, ROWS, WIDTH), f32),
             pltpu.VMEM((CHUNKS, ROWS, WIDTH), f32),
             dma((CHUNKS,)),
             dma((CHUNKS,)),
-            pltpu.SMEM((1,), f32),
+            pltpu.VMEM((1, 1), f32),
             dma(()),
             pltpu.VMEM((1, ROWS), f32),
             pltpu.VMEM((1, ROWS), f32),
@@ -266,36 +266,39 @@
             dma(()),
             pltpu.VMEM((4, 1, WIDTH), f32),
             pltpu.VMEM((4, 1, (CHUNKS - 1) * WIDTH), f32),
-            pltpu.VMEM((2, 1, COLS), f32),
             dma((2, 3)),
             dma((2, 3)),
-            pltpu.VMEM((2, 4 * ROWS, COLS), bf16),
-            dma((CHUNKS,)),
-            dma((CHUNKS,)),
-            dma((CHUNKS,)),
-            dma((CHUNKS,)),
-            dma((CHUNKS,)),
-            dma((CHUNKS,)),
-            dma((4, CHUNKS)),
-            dma((1,)),
+            dma((CHUNKS,)),
+            dma((CHUNKS,)),
+            dma((CHUNKS,)),
+            dma((CHUNKS,)),
+            dma((CHUNKS,)),
+            dma((CHUNKS,)),
             pltpu.VMEM((4, 4, 128), f32),
             pltpu.VMEM((64, RB, 128), f32),
-            pltpu.VMEM((64, RB * 128), bf16),
             dma((3,)),
             dma((3,)),
             dma((2, 1)),
             dma((2, 3)),
             dma((2, 7)),
-            dma((3,)),
         ],
         compiler_params=pltpu.CompilerParams(
-            collective_id=0, has_side_effects=True, vmem_limit_bytes=67043328
+            collective_id=0, has_side_effects=True, vmem_limit_bytes=53 * 1024 * 1024
         ),
         name="mean_and_gather",
     )(
-        w_gate[0], avg_gate[0], w_up[0], avg_up[0], mix_share,
+        w_gate[0], avg_gate[0], w_up[0], avg_up[0], mix_share[:, None],
         router_weight.T, router_gain[None, :],
     )
+    outs = pl.pallas_call(
+        put_out,
+        out_shape=shapes,
+        in_specs=[pl.BlockSpec(memory_space=pltpu.VMEM)] * 5,
+        out_specs=[anywhere] * 5,
+        scratch_shapes=[dma((11,))],
+        compiler_params=pltpu.CompilerParams(vmem_limit_bytes=1024 * 1024),
+        name="put_out",
+    )(*outs)
     gate, up, sgate, sup, router = outs
     return gate[None], up[None], sgate, sup, router.T
 

time: 91.3 us -> 87.8 us (0.962)
  local copies, waits for them, and re-layouts: 8.73 us -> 0 us
  Pallas kernels: 81.1 us -> 86.4 us
    unnamed x13 -> x0, local copies, waits for them, and re-layouts: 8.73 us -> none
    pallas_call x1 -> x2, Pallas kernels: 81.1 us -> 86.4 us  [the longest x1 82.9 us: local(): pl.pallas_call(kernel, out_shape=held, in_specs=[anywhere] * 7, out_specs...]
where the time goes in v2:
time: 87.8 us; the launch traced here: 87.6 us
  Pallas kernels  86.4 us (98%)
  between operations  1.29 us (1%)
    pallas_call x1, Pallas kernels, local(): pl.pallas_call(kernel, out_shape=held, in_specs=[anywhere] * 7, out_specs...  82.9 us
    pallas_call x1, Pallas kernels, local(): pl.pallas_call(put_out, out_shape=shapes, in_specs=[pl.BlockSpec(memory_s...  3.45 us

profile of v2, /device:TPU:8, one launch (start us, length us, event | category | flops | bytes accessed | tf_op | source)
XLA Modules:
  0.0 87.6 jit_solution(17494172927949834998)
XLA Ops:
  1.3 82.9 %mean_and_gather.1 = (bf16[2048,1024]{1,0:T(8,128)(2,1)S(1)}, bf16[2048,1024]{1,0:T(8,128)(2,1)S(1)}, f32[1,1024]{1,0:T(1,128)S(1)}, f32[1,1024]{1,0:T(1,128)S(1)}, bf16[64,2048]{1,0:T(8,128)(2,1)S(1)}) custom-call(f32[512,1024]{1,0:T(8,128)} %bitcast.11, f32[512,1024]{1,0:T(8,128)} %bitcast.12, f32[512,1024]{1,0:T(8,128)} %bitcast.13, ...), custom_call_target="tpu_custom_call" | custom-call | tf_op jit(solution)/shard_map/mean_and_gather/pallas_call | solution.py:251
  84.2 3.4 %put_out.1 = (bf16[2048,1024]{1,0:T(8,128)(2,1)}, bf16[2048,1024]{1,0:T(8,128)(2,1)}, f32[1,1024]{1,0:T(1,128)}, f32[1,1024]{1,0:T(1,128)}, bf16[64,2048]{1,0:T(8,128)(2,1)}) custom-call(bf16[2048,1024]{1,0:T(8,128)(2,1)S(1)} %get-tuple-element.15.gate, bf16[2048,1024]{1,0:T(8,128)(2,1)S(1)} %get-tuple-element.16.up, f32[1,1024]{1,0:T(1,128)S(1)} %get-tuple-element.17.sgate, ...), custom_call_target="tpu_custom_call" | custom-call | tf_op jit(solution)/shard_map/put_out/pallas_call | solution.py:293

commit v3 on v2

--- a/solution.py
+++ b/solution.py
@@ -13,15 +13,16 @@
 CHUNKS = 2 * PER
 STEP = 64
 RB = 16
+EARLY = 2
 
 
 def kernel(
     w_gate, avg_gate, w_up, avg_up, mix, router_w, router_g,
     o_gate, o_up, o_sgate, o_sup, o_router,
-    wide, other, wide_sem, other_sem, mix_s, mix_sem, rw, rg, rw_sem, rg_sem,
+    wide, other, wide_sem, other_sem, rw, rg, rw_sem, rg_sem,
     sums0, sums1, sums_send, sums_recv,
     send_r, send_l, recv_l, recv_r, fsend, frecv,
-    xr, bank_r, rx_send, rx_recv, rc, ry, rz,
+    xr, bank_r, rx_send, rx_recv, rc, ry, rz, joined, ready, go,
 ):
     bank = lax.axis_index("bank")
     me = lax.axis_index("zero")
@@ -36,34 +37,48 @@
     twin = at_bank(zz, yy, 1 - core)
     y_up, y_down = at_bank(zz, lax.rem(yy + 1, 4), core), at_bank(zz, lax.rem(yy + 3, 4), core)
     z_up, z_down = at_bank(lax.rem(zz + 1, 8), yy, core), at_bank(lax.rem(zz + 7, 8), yy, core)
-
     outs, scales = (o_gate, o_up), (o_sgate, o_sup)
     w_in, a_in = (w_gate, w_up), (avg_gate, avg_up)
 
-    mix_copy = pltpu.make_async_copy(mix, mix_s, mix_sem)
-    mix_copy.start()
     loads = []
     for c in range(CHUNKS):
         m, cols = c // PER, pl.ds((c % PER) * WIDTH, WIDTH)
-        first = pltpu.make_async_copy(w_in[m].at[:, cols], wide.at[c], wide_sem.at[c])
-        second = pltpu.make_async_copy(a_in[m].at[:, cols], other.at[c], other_sem.at[c])
-        first.start()
-        second.start()
-        loads.append((first, second))
+        loads.append((
+            pltpu.make_async_copy(w_in[m].at[:, cols], wide.at[c], wide_sem.at[c]),
+            pltpu.make_async_copy(a_in[m].at[:, cols], other.at[c], other_sem.at[c]),
+        ))
     load_rw = pltpu.make_async_copy(router_w, rw, rw_sem)
     load_rg = pltpu.make_async_copy(router_g, rg, rg_sem)
-    load_rw.start()
-    load_rg.start()
+
+    def start_loads(first, last):
+        for c in range(first, last):
+            for copy in loads[c]:
+                copy.start()
+
+    start_loads(0, EARLY)
 
     barrier = pltpu.get_barrier_semaphore()
-    for where in (
-        (bank, right), (bank, left), (bank, across),
-        (twin, me), (y_up, me), (y_down, me), (z_up, me), (z_down, me),
-    ):
-        pl.semaphore_signal(barrier, inc=1, device_id=where, device_id_type=MESH)
-
-    mix_copy.wait()
-    share = mix_s[...]
+    lead = me == 0
+    for step in range(1, 4):
+        @pl.when(me + step < 4)
+        def _():
+            pl.semaphore_signal(barrier, inc=1, device_id=(bank, lax.rem(me + step, 4)), device_id_type=MESH)
+
+    beside = (twin, y_up, y_down, z_up, z_down)
+
+    @pl.when(lead)
+    def _():
+        for where in beside:
+            pl.semaphore_signal(barrier, inc=1, device_id=(where, 0), device_id_type=MESH)
+
+    for i in range(1, 4):
+        @pl.when(me == i)
+        def _():
+            pl.semaphore_wait(barrier, i)
+            for j in range(i):
+                pl.semaphore_signal(joined, inc=1, device_id=(bank, j), device_id_type=MESH)
+
+    share = jnp.full((8, WIDTH), mix[0], jnp.float32)
     rest = 1.0 - share
 
     def mixed(c):
@@ -71,31 +86,44 @@
         loads[c][1].wait()
 
         def step(i, acc):
-            rows = pl.ds(i * STEP, STEP)
-            fresh = share * wide[c, rows, :] + rest * other[c, rows, :]
-            wide[c, rows, :] = fresh
-            return acc + jnp.sum((fresh * fresh).reshape(STEP // 8, 8, WIDTH), axis=0)
-
-        acc = lax.fori_loop(0, ROWS // STEP, step, jnp.zeros((8, WIDTH), jnp.float32))
-        return jnp.sum(acc, axis=0, keepdims=True)
+            for k in range(STEP // 8):
+                rows = pl.ds(pl.multiple_of(i * STEP + 8 * k, 8), 8)
+                fresh = share * wide[c, rows, :] + rest * other[c, rows, :]
+                wide[c, rows, :] = fresh
+                acc[k % 4] += fresh * fresh
+            return acc
+
+        acc = lax.fori_loop(0, ROWS // STEP, step, [jnp.zeros((8, WIDTH), jnp.float32)] * 4)
+        return jnp.sum((acc[0] + acc[1]) + (acc[2] + acc[3]), axis=0, keepdims=True)
 
     peers = (right, left, across)
 
     def share_sums(buf, g):
         copies = []
-        for k, peer in enumerate(peers):
+        for k in (2, 0, 1):
             copy = pltpu.make_async_remote_copy(
                 src_ref=buf.at[me], dst_ref=buf.at[me],
                 send_sem=sums_send.at[g, k], recv_sem=sums_recv.at[g, k],
-                device_id=(bank, peer), device_id_type=MESH,
+                device_id=(bank, peers[k]), device_id_type=MESH,
             )
             copy.start()
             copies.append(copy)
         return copies
 
     sums0[me] = mixed(0)
-    pl.semaphore_wait(barrier, 8)
+    start_loads(EARLY, CHUNKS)
+    load_rw.start()
+    load_rg.start()
+    for i in range(3):
+        @pl.when(me == i)
+        def _():
+            pl.semaphore_wait(joined, 3 - i)
+
     sent0 = share_sums(sums0, 0)
+
+    for c in range(1, CHUNKS):
+        sums1[me, :, pl.ds((c - 1) * WIDTH, WIDTH)] = mixed(c)
+    sent1 = share_sums(sums1, 1)
 
     load_rw.wait()
     load_rg.wait()
@@ -112,10 +140,6 @@
         copy.start()
         sent_x.append(copy)
 
-    for c in range(1, CHUNKS):
-        sums1[me, :, pl.ds((c - 1) * WIDTH, WIDTH)] = mixed(c)
-    sent1 = share_sums(sums1, 1)
-
     def where_at(c, owner):
         return outs[c // PER].at[pl.ds(owner * ROWS, ROWS), pl.ds((c % PER) * WIDTH, WIDTH)]
 
@@ -123,14 +147,14 @@
 
     def normalised(c):
         s = scales[c // PER][:, pl.ds((c % PER) * WIDTH, WIDTH)]
-        inverse = 1.0 / s
+        inverse = jnp.broadcast_to(1.0 / s, (16, WIDTH))
 
         def step(i, carry):
-            rows = pl.ds(i * STEP, STEP)
-            outs[c // PER][
-                pl.ds(pl.multiple_of(me * ROWS + i * STEP, STEP), STEP),
-                pl.ds((c % PER) * WIDTH, WIDTH),
-            ] = (wide[c, rows, :] * inverse).astype(jnp.bfloat16)
+            for k in range(STEP // 16):
+                outs[c // PER][
+                    pl.ds(pl.multiple_of(me * ROWS + i * STEP + 16 * k, 16), 16),
+                    pl.ds((c % PER) * WIDTH, WIDTH),
+                ] = (wide[c, pl.ds(pl.multiple_of(i * STEP + 16 * k, 16), 16), :] * inverse).astype(jnp.bfloat16)
             return carry
 
         lax.fori_loop(0, ROWS // STEP, step, 0)
@@ -154,6 +178,19 @@
     o_sup[...] = total[:, COLS - WIDTH :]
     for c in range(1, CHUNKS):
         normalised(c)
+
+    @pl.when(lead)
+    def _():
+        pl.semaphore_wait(barrier, len(beside))
+        for where in beside:
+            pl.semaphore_signal(ready, inc=1, device_id=(where, 0), device_id_type=MESH)
+        pl.semaphore_wait(ready, len(beside))
+        for j in range(1, 4):
+            pl.semaphore_signal(go, inc=1, device_id=(bank, j), device_id_type=MESH)
+
+    @pl.when(me > 0)
+    def _():
+        pl.semaphore_wait(go, 1)
 
     for copy in sent_x:
         copy.wait_recv()
@@ -231,35 +268,24 @@
 
 
 def local(w_gate, avg_gate, w_up, avg_up, mix_share, router_weight, router_gain):
-    dma = pltpu.SemaphoreType.DMA
+    dma, regular = pltpu.SemaphoreType.DMA, pltpu.SemaphoreType.REGULAR
     f32, bf16 = jnp.float32, jnp.bfloat16
     anywhere = pl.BlockSpec(memory_space=pl.ANY)
-    shapes = (
-            jax.ShapeDtypeStruct((4 * ROWS, COLS), bf16),
-            jax.ShapeDtypeStruct((4 * ROWS, COLS), bf16),
-            jax.ShapeDtypeStruct((1, COLS), f32),
-            jax.ShapeDtypeStruct((1, COLS), f32),
-            jax.ShapeDtypeStruct((64, RB * 128), bf16),
+    in_vmem = pl.BlockSpec(memory_space=pltpu.VMEM)
+    results = (
+        ((4 * ROWS, COLS), bf16), ((4 * ROWS, COLS), bf16),
+        ((1, COLS), f32), ((1, COLS), f32), ((64, RB * 128), bf16),
     )
-    held = (
-            pltpu.VMEM((4 * ROWS, COLS), bf16),
-            pltpu.VMEM((4 * ROWS, COLS), bf16),
-            pltpu.VMEM((1, COLS), f32),
-            pltpu.VMEM((1, COLS), f32),
-            pltpu.VMEM((64, RB * 128), bf16),
-    )
-    outs = pl.pallas_call(
+    held = pl.pallas_call(
         kernel,
-        out_shape=held,
-        in_specs=[anywhere] * 7,
-        out_specs=[pl.BlockSpec(memory_space=pltpu.VMEM)] * 5,
+        out_shape=tuple(pltpu.VMEM(*r) for r in results),
+        in_specs=[anywhere] * 4 + [pl.BlockSpec(memory_space=pltpu.SMEM)] + [anywhere] * 2,
+        out_specs=[in_vmem] * 5,
         scratch_shapes=[
             pltpu.VMEM((CHUNKS, ROWS, WIDTH), f32),
             pltpu.VMEM((CHUNKS, ROWS, WIDTH), f32),
             dma((CHUNKS,)),
             dma((CHUNKS,)),
-            pltpu.VMEM((1, 1), f32),
-            dma(()),
             pltpu.VMEM((1, ROWS), f32),
             pltpu.VMEM((1, ROWS), f32),
             dma(()),
@@ -281,25 +307,27 @@
             dma((2, 1)),
             dma((2, 3)),
             dma((2, 7)),
+            regular,
+            regular,
+            regular,
         ],
         compiler_params=pltpu.CompilerParams(
             collective_id=0, has_side_effects=True, vmem_limit_bytes=53 * 1024 * 1024
         ),
         name="mean_and_gather",
     )(
-        w_gate[0], avg_gate[0], w_up[0], avg_up[0], mix_share[:, None],
+        w_gate[0], avg_gate[0], w_up[0], avg_up[0], mix_share,
         router_weight.T, router_gain[None, :],
     )
-    outs = pl.pallas_call(
+    gate, up, sgate, sup, router = pl.pallas_call(
         put_out,
-        out_shape=shapes,
-        in_specs=[pl.BlockSpec(memory_space=pltpu.VMEM)] * 5,
+        out_shape=tuple(jax.ShapeDtypeStruct(*r) for r in results),
+        in_specs=[in_vmem] * 5,
         out_specs=[anywhere] * 5,
         scratch_shapes=[dma((11,))],
         compiler_params=pltpu.CompilerParams(vmem_limit_bytes=1024 * 1024),
         name="put_out",
-    )(*outs)
-    gate, up, sgate, sup, router = outs
+    )(*held)
     return gate[None], up[None], sgate, sup, router.T
 
 

time: 87.8 us -> 82.3 us (0.937)
  Pallas kernels: 86.4 us -> 80.9 us
    pallas_call x2, Pallas kernels: 86.4 us -> 80.9 us  [the longest x1 77.5 us: local(): pl.pallas_call(kernel, out_shape=tuple((pltpu.VMEM(*r) for r in results))...]
where the time goes in v3:
time: 82.3 us; the launch traced here: 82.2 us
  Pallas kernels  80.9 us (98%)
  between operations  1.29 us (2%)
    pallas_call x1, Pallas kernels, local(): pl.pallas_call(kernel, out_shape=tuple((pltpu.VMEM(*r) for r in results))...  77.5 us
    pallas_call x1, Pallas kernels, local(): pl.pallas_call(put_out, out_shape=tuple((jax.ShapeDtypeStruct(*r) for r i...  3.45 us

profile of v3, /device:TPU:8, one launch (start us, length us, event | category | flops | bytes accessed | tf_op | source)
XLA Modules:
  0.0 82.2 jit_solution(9627231557687191373)
XLA Ops:
  1.3 77.5 %mean_and_gather.1 = (bf16[2048,1024]{1,0:T(8,128)(2,1)S(1)}, bf16[2048,1024]{1,0:T(8,128)(2,1)S(1)}, f32[1,1024]{1,0:T(1,128)S(1)}, f32[1,1024]{1,0:T(1,128)S(1)}, bf16[64,2048]{1,0:T(8,128)(2,1)S(1)}) custom-call(f32[512,1024]{1,0:T(8,128)} %bitcast.9, f32[512,1024]{1,0:T(8,128)} %bitcast.10, f32[512,1024]{1,0:T(8,128)} %bitcast.11, f32[512,1024]{1,0:T(8,128)} %bitcast.12, ...), custom_call_target="tpu_custom_call" | custom-call | tf_op jit(solution)/shard_map/mean_and_gather/pallas_call | solution.py:279
  78.8 3.4 %put_out.1 = (bf16[2048,1024]{1,0:T(8,128)(2,1)}, bf16[2048,1024]{1,0:T(8,128)(2,1)}, f32[1,1024]{1,0:T(1,128)}, f32[1,1024]{1,0:T(1,128)}, bf16[64,2048]{1,0:T(8,128)(2,1)}) custom-call(bf16[2048,1024]{1,0:T(8,128)(2,1)S(1)} %get-tuple-element.15.gate, bf16[2048,1024]{1,0:T(8,128)(2,1)S(1)} %get-tuple-element.16.up, f32[1,1024]{1,0:T(1,128)S(1)} %get-tuple-element.17.sgate, ...), custom_call_target="tpu_custom_call" | custom-call | tf_op jit(solution)/shard_map/put_out/pallas_call | solution.py:322

commit v4 on v3

v4 whole, which is shorter than its diff:
```python
import jax
import jax.numpy as jnp
from jax import lax
from jax.experimental import pallas as pl
from jax.experimental.pallas import tpu as pltpu
from jax.sharding import PartitionSpec as P

MESH = pl.DeviceIdType.MESH
ROWS = 512
COLS = 1024
WIDTH = 256
HALF = WIDTH // 2
PER = COLS // WIDTH
STEP = 128
RB = 16
RAW = 320
LOADS = ((0, 0, WIDTH), (0, WIDTH, WIDTH), (0, 2 * WIDTH, 2 * WIDTH), (1, 0, 2 * WIDTH), (1, 2 * WIDTH, 2 * WIDTH))


def kernel(
    w_gate, avg_gate, w_up, avg_up, mix, router_w, router_g,
    o_gate, o_up, o_sgate, o_sup, o_router,
    wide, other, load_sem, router_in, router_sem,
    sums0, sums1, sums2, sums_send, sums_recv, raw_in, raw_send, raw_recv,
    bulk_send, gate_recv, up_recv, late_recv, pass_send, pass_recv,
    xr, bank_r, x_send, x_recv, b_send, twin_recv, y_recv, z_recv, joined, ready, go,
):
    bank = lax.axis_index("bank")
    me = lax.axis_index("zero")
    right, left, across = lax.rem(me + 1, 4), lax.rem(me + 3, 4), lax.rem(me + 2, 4)
    core = lax.rem(bank, 2)
    yy = lax.rem(bank // 2, 4)
    zz = bank // 8

    def at_bank(z, y, c):
        return (z * 4 + y) * 2 + c

    twin = at_bank(zz, yy, 1 - core)
    y_up, y_down = at_bank(zz, lax.rem(yy + 1, 4), core), at_bank(zz, lax.rem(yy + 3, 4), core)
    z_up, z_down = at_bank(lax.rem(zz + 1, 8), yy, core), at_bank(lax.rem(zz + 7, 8), yy, core)
    outs, scales = (o_gate, o_up), (o_sgate, o_sup)
    w_in, a_in = (w_gate, w_up), (avg_gate, avg_up)

    def remote(src, dst, send, recv, where, who):
        return pltpu.make_async_remote_copy(
            src_ref=src, dst_ref=dst, send_sem=send, recv_sem=recv,
            device_id=(where, who), device_id_type=MESH,
        )

    def arrived(ref, sem):
        remote(ref, ref, sem, sem, bank, right).wait_recv()

    def departed(ref, sem):
        remote(ref, ref, sem, sem, bank, right).wait_send()

    def start_load(k):
        m, first, count = LOADS[k]
        cols = pl.ds(first, count)
        pltpu.make_async_copy(w_in[m].at[:, cols], wide.at[m, :, cols], load_sem.at[k]).start()
        pltpu.make_async_copy(a_in[m].at[:, cols], other.at[m, :, cols], load_sem.at[k]).start()

    def loaded(k):
        both = pl.ds(0, 2 * LOADS[k][2])
        pltpu.make_async_copy(w_gate.at[:, both], wide.at[0, :, both], load_sem.at[k]).wait()

    start_load(0)
    start_load(1)

    barrier = pltpu.get_barrier_semaphore()
    lead = me == 0
    beside = (twin, y_up, y_down, z_up, z_down)

    def greet(where, who):
        pl.semaphore_signal(barrier, inc=1, device_id=(where, who), device_id_type=MESH)

    for step in range(1, 4):
        @pl.when(me + step < 4)
        def _():
            greet(bank, lax.rem(me + step, 4))

    @pl.when(lead)
    def _():
        for where in beside:
            greet(where, 0)

    for i in range(1, 4):
        @pl.when(me == i)
        def _():
            pl.semaphore_wait(barrier, i)
            for j in range(i):
                pl.semaphore_signal(joined, inc=1, device_id=(bank, j), device_id_type=MESH)

    share = jnp.full((8, WIDTH), mix[0], jnp.float32)
    rest = 1.0 - share

    def mixed(c):
        m, cols = c // PER, pl.ds((c % PER) * WIDTH, WIDTH)

        def step(i, acc):
            for k in range(STEP // 8):
                rows = pl.ds(pl.multiple_of(i * STEP + 8 * k, 8), 8)
                fresh = share * wide[m, rows, cols] + rest * other[m, rows, cols]
                wide[m, rows, cols] = fresh
                acc[k % 4] += fresh * fresh
            return acc

        acc = lax.fori_loop(0, ROWS // STEP, step, [jnp.zeros((8, WIDTH), jnp.float32)] * 4)
        return jnp.sum((acc[0] + acc[1]) + (acc[2] + acc[3]), axis=0, keepdims=True)

    peers = (across, right, left)

    def share_sums(buf, k):
        for peer in peers:
            remote(buf.at[me], buf.at[me], sums_send, sums_recv.at[k], bank, peer).start()

    def totals(buf, k):
        arrived(buf.at[pl.ds(0, 3)], sums_recv.at[k])
        return jnp.sqrt(((buf[0] + buf[1]) + buf[2]) + buf[3])

    loaded(0)
    sums0[me] = mixed(0)
    start_load(2)
    start_load(3)
    start_load(4)
    pltpu.make_async_copy(router_w, router_in.at[pl.ds(0, 1)], router_sem).start()
    pltpu.make_async_copy(router_g, router_in.at[pl.ds(1, 1)], router_sem).start()

    for i in range(3):
        @pl.when(me == i)
        def _():
            pl.semaphore_wait(joined, 3 - i)

    share_sums(sums0, 0)

    def send_raw(k):
        rows = pl.ds(k * RAW // 2, RAW // 2)
        for side, dest in enumerate((right, left)):
            remote(wide.at[0, rows, pl.ds(0, HALF)], raw_in.at[side, rows], raw_send, raw_recv, bank, dest).start()

    send_raw(0)
    loaded(1)
    sums1[me, :, pl.ds(0, WIDTH)] = mixed(1)
    loaded(2)
    for c in range(2, PER):
        sums1[me, :, pl.ds((c - 1) * WIDTH, WIDTH)] = mixed(c)
    share_sums(sums1, 1)
    send_raw(1)
    for k in (3, 4):
        loaded(k)
        for c in (2 * k - 2, 2 * k - 1):
            sums2[me, :, pl.ds((c - PER) * WIDTH, WIDTH)] = mixed(c)
    share_sums(sums2, 2)

    pltpu.make_async_copy(w_gate.at[pl.ds(0, 2), pl.ds(0, ROWS)], router_in, router_sem).wait()
    prod = router_in[0:1, :] * router_in[1:2, :]
    for k in range(4):
        xr[me, pl.ds(k, 1), :] = prod[:, k * 128 : (k + 1) * 128]
    for peer in peers:
        remote(xr.at[me], xr.at[me], x_send, x_recv, bank, peer).start()

    def where_at(c, owner):
        return outs[c // PER].at[pl.ds(owner * ROWS, ROWS), pl.ds((c % PER) * WIDTH, WIDTH)]

    def normalised(c):
        cols = pl.ds((c % PER) * WIDTH, WIDTH)
        inverse = jnp.broadcast_to(1.0 / scales[c // PER][:, cols], (16, WIDTH))

        def step(i, carry):
            for k in range(STEP // 16):
                rows = pl.ds(pl.multiple_of(i * STEP + 16 * k, 16), 16)
                outs[c // PER][pl.ds(pl.multiple_of(me * ROWS + i * STEP + 16 * k, 16), 16), cols] = (
                    wide[c // PER, rows, cols] * inverse
                ).astype(jnp.bfloat16)
            return carry

        lax.fori_loop(0, ROWS // STEP, step, 0)

    def send_both(block, from_left, from_right):
        remote(block, block, bulk_send, from_left, bank, right).start()
        remote(block, block, bulk_send, from_right, bank, left).start()

    o_sgate[:, pl.ds(0, WIDTH)] = totals(sums0, 0)
    normalised(0)
    send_both(o_gate.at[pl.ds(me * ROWS, ROWS), pl.ds(HALF, HALF)], gate_recv.at[0], gate_recv.at[1])
    send_both(o_gate.at[pl.ds(me * ROWS + RAW, ROWS - RAW), pl.ds(0, HALF)], gate_recv.at[0], gate_recv.at[1])
    o_sgate[:, pl.ds(WIDTH, COLS - WIDTH)] = totals(sums1, 1)
    for c in range(1, PER):
        normalised(c)
        send_both(where_at(c, me), gate_recv.at[0], gate_recv.at[1])
    o_sup[...] = totals(sums2, 2)
    for c in range(PER, 2 * PER):
        normalised(c)
        send_both(where_at(c, me), late_recv, up_recv.at[0 if c < 2 * PER - 1 else 1])

    @pl.when(lead)
    def _():
        pl.semaphore_wait(barrier, 5)
        for where in beside:
            pl.semaphore_signal(ready, inc=1, device_id=(where, 0), device_id_type=MESH)
        pl.semaphore_wait(ready, 5)
        for j in range(1, 4):
            pl.semaphore_signal(go, inc=1, device_id=(bank, j), device_id_type=MESH)

    @pl.when(jnp.logical_not(lead))
    def _():
        pl.semaphore_wait(go, 1)

    arrived(xr.at[pl.ds(0, 3)], x_recv)
    for k in range(4):
        bank_r[bank, pl.ds(4 * k, 4), :] = xr[k]

    def push(first, count, dest, recv):
        block = bank_r.at[pl.ds(first, count)]
        remote(block, block, b_send, recv, dest, me).start()

    def got(count, recv):
        arrived(bank_r.at[pl.ds(0, count)], recv)

    push(bank, 1, twin, twin_recv)
    got(1, twin_recv)
    pair = at_bank(zz, yy, 0)
    push(pair, 2, y_up, y_recv.at[0])
    push(pair, 2, y_down, y_recv.at[1])
    got(2, y_recv.at[0])
    push(at_bank(zz, lax.rem(yy + 3, 4), 0), 2, y_up, y_recv.at[1])
    got(4, y_recv.at[1])
    push(zz * 8, 8, z_up, z_recv.at[0])
    push(zz * 8, 8, z_down, z_recv.at[3])
    for k in range(1, 4):
        got(8, z_recv.at[k - 1])
        push(lax.rem(zz + 8 - k, 8) * 8, 8, z_up, z_recv.at[k if k < 3 else 5])
        if k < 3:
            got(8, z_recv.at[k + 2])
            push(lax.rem(zz + k, 8) * 8, 8, z_down, z_recv.at[k + 3])
    got(16, z_recv.at[5])
    for k in range(RB):
        o_router[:, k * 128 : (k + 1) * 128] = bank_r[:, k, :].astype(jnp.bfloat16)

    arrived(raw_in, raw_recv)
    inverse = jnp.broadcast_to(1.0 / o_sgate[:, pl.ds(0, HALF)], (16, HALF))
    for side, owner in enumerate((left, right)):
        for k in range(RAW // 16):
            o_gate[pl.ds(pl.multiple_of(owner * ROWS + 16 * k, 16), 16), pl.ds(0, HALF)] = (
                raw_in[side, pl.ds(16 * k, 16), :] * inverse
            ).astype(jnp.bfloat16)

    short = RAW * HALF // COLS
    arrived(o_gate.at[pl.ds(0, ROWS - short)], gate_recv.at[0])
    block = o_gate.at[pl.ds(left * ROWS, ROWS)]
    remote(block, block, pass_send, pass_recv.at[0], bank, right).start()
    for k, (first, count) in enumerate(((0, COLS - WIDTH), (COLS - WIDTH, WIDTH))):
        block = o_up.at[pl.ds(right * ROWS, ROWS), pl.ds(first, count)]
        arrived(block, up_recv.at[k])
        remote(block, block, pass_send, pass_recv.at[1], bank, left).start()

    arrived(o_gate.at[pl.ds(0, ROWS - short)], gate_recv.at[1])
    arrived(o_up.at[pl.ds(0, ROWS)], late_recv)
    departed(raw_in.at[0, pl.ds(0, 48)], sums_send)
    departed(raw_in, raw_send)
    departed(xr.at[pl.ds(0, 3)], x_send)
    departed(bank_r.at[pl.ds(0, 63)], b_send)
    departed(o_gate.at[pl.ds(0, 4 * ROWS - 2 * short)], bulk_send)
    arrived(o_gate.at[pl.ds(0, ROWS)], pass_recv.at[0])
    arrived(o_up.at[pl.ds(0, ROWS)], pass_recv.at[1])
    departed(o_gate.at[pl.ds(0, 2 * ROWS)], pass_send)


def put_out(gate, up, sgate, sup, router, o_gate, o_up, o_sgate, o_sup, o_router, sem):
    copies = []
    for i, (a, b) in enumerate(((gate, o_gate), (up, o_up))):
        for k in range(4):
            rows = pl.ds(k * ROWS, ROWS)
            copies.append(pltpu.make_async_copy(a.at[rows], b.at[rows], sem.at[4 * i + k]))
    copies.append(pltpu.make_async_copy(router, o_router, sem.at[8]))
    copies.append(pltpu.make_async_copy(sgate, o_sgate, sem.at[9]))
    copies.append(pltpu.make_async_copy(sup, o_sup, sem.at[10]))
    for copy in copies:
        copy.start()
    for copy in copies:
        copy.wait()


def local(w_gate, avg_gate, w_up, avg_up, mix_share, router_weight, router_gain):
    dma, regular = pltpu.SemaphoreType.DMA, pltpu.SemaphoreType.REGULAR
    f32, bf16 = jnp.float32, jnp.bfloat16
    anywhere = pl.BlockSpec(memory_space=pl.ANY)
    in_vmem = pl.BlockSpec(memory_space=pltpu.VMEM)
    results = (
        ((4 * ROWS, COLS), bf16), ((4 * ROWS, COLS), bf16),
        ((1, COLS), f32), ((1, COLS), f32), ((64, RB * 128), bf16),
    )
    held = pl.pallas_call(
        kernel,
        out_shape=tuple(pltpu.VMEM(*r) for r in results),
        in_specs=[anywhere] * 4 + [pl.BlockSpec(memory_space=pltpu.SMEM)] + [anywhere] * 2,
        out_specs=[in_vmem] * 5,
        scratch_shapes=[
            pltpu.VMEM((2, ROWS, COLS), f32),
            pltpu.VMEM((2, ROWS, COLS), f32),
            dma((len(LOADS),)),
            pltpu.VMEM((2, ROWS), f32),
            dma(()),
            pltpu.VMEM((4, 1, WIDTH), f32),
            pltpu.VMEM((4, 1, COLS - WIDTH), f32),
            pltpu.VMEM((4, 1, COLS), f32),
            dma(()),
            dma((3,)),
            pltpu.VMEM((2, RAW, HALF), f32),
            dma(()),
            dma(()),
            dma(()),
            dma((2,)),
            dma((2,)),
            dma(()),
            dma(()),
            dma((2,)),
            pltpu.VMEM((4, 4, 128), f32),
            pltpu.VMEM((64, RB, 128), f32),
            dma(()),
            dma(()),
            dma(()),
            dma(()),
            dma((2,)),
            dma((6,)),
            regular,
            regular,
            regular,
        ],
        compiler_params=pltpu.CompilerParams(
            collective_id=0, has_side_effects=True, vmem_limit_bytes=53 * 1024 * 1024
        ),
        name="mean_and_gather",
    )(
        w_gate[0], avg_gate[0], w_up[0], avg_up[0], mix_share,
        router_weight.T, router_gain[None, :],
    )
    gate, up, sgate, sup, router = pl.pallas_call(
        put_out,
        out_shape=tuple(jax.ShapeDtypeStruct(*r) for r in results),
        in_specs=[in_vmem] * 5,
        out_specs=[anywhere] * 5,
        scratch_shapes=[dma((11,))],
        compiler_params=pltpu.CompilerParams(vmem_limit_bytes=1024 * 1024),
        name="put_out",
    )(*held)
    return gate[None], up[None], sgate, sup, router.T


def solution(mesh):
    placed = (
        P("bank", "zero", None),
        P("bank", "zero", None),
        P("bank", "zero", None),
        P("bank", "zero", None),
        P("bank"),
        P("zero", "bank"),
        P("zero"),
    )
    return jax.shard_map(
        local,
        mesh=mesh,
        in_specs=placed,
        out_specs=(
            P("bank", None, None),
            P("bank", None, None),
            P("bank", None),
            P("bank", None),
            P(),
        ),
        check_vma=False,
    )
```

time: 82.3 us -> 80.5 us (0.978)
  Pallas kernels: 80.9 us -> 79.1 us
    pallas_call x1, Pallas kernels: 77.5 us -> 75.6 us  [local(): pl.pallas_call(kernel, out_shape=tuple((pltpu.VMEM(*r) for r in results))...]
where the time goes in v4:
time: 80.5 us; the launch traced here: 80.4 us
  Pallas kernels  79.1 us (98%)
  between operations  1.29 us (2%)
    pallas_call x1, Pallas kernels, local(): pl.pallas_call(kernel, out_shape=tuple((pltpu.VMEM(*r) for r in results))...  75.6 us
    pallas_call x1, Pallas kernels, local(): pl.pallas_call(put_out, out_shape=tuple((jax.ShapeDtypeStruct(*r) for r i...  3.45 us

profile of v4, /device:TPU:8, one launch (start us, length us, event | category | flops | bytes accessed | tf_op | source)
XLA Modules:
  0.0 80.4 jit_solution(9694525556824807572)
XLA Ops:
  1.3 75.6 %mean_and_gather.1 = (bf16[2048,1024]{1,0:T(8,128)(2,1)S(1)}, bf16[2048,1024]{1,0:T(8,128)(2,1)S(1)}, f32[1,1024]{1,0:T(1,128)S(1)}, f32[1,1024]{1,0:T(1,128)S(1)}, bf16[64,2048]{1,0:T(8,128)(2,1)S(1)}) custom-call(f32[512,1024]{1,0:T(8,128)} %bitcast.9, f32[512,1024]{1,0:T(8,128)} %bitcast.10, f32[512,1024]{1,0:T(8,128)} %bitcast.11, f32[512,1024]{1,0:T(8,128)} %bitcast.12, ...), custom_call_target="tpu_custom_call" | custom-call | tf_op jit(solution)/shard_map/mean_and_gather/pallas_call | solution.py:292
  76.9 3.4 %put_out.1 = (bf16[2048,1024]{1,0:T(8,128)(2,1)}, bf16[2048,1024]{1,0:T(8,128)(2,1)}, f32[1,1024]{1,0:T(1,128)}, f32[1,1024]{1,0:T(1,128)}, bf16[64,2048]{1,0:T(8,128)(2,1)}) custom-call(bf16[2048,1024]{1,0:T(8,128)(2,1)S(1)} %get-tuple-element.15.gate, bf16[2048,1024]{1,0:T(8,128)(2,1)S(1)} %get-tuple-element.16.up, f32[1,1024]{1,0:T(1,128)S(1)} %get-tuple-element.17.sgate, ...), custom_call_target="tpu_custom_call" | custom-call | tf_op jit(solution)/shard_map/put_out/pallas_call | solution.py:337

commit v5 on v4

--- a/solution.py
+++ b/solution.py
@@ -14,6 +14,8 @@
 STEP = 128
 RB = 16
 RAW = 320
+FIRST = (768, 128)
+REST = COLS - min(FIRST)
 LOADS = ((0, 0, WIDTH), (0, WIDTH, WIDTH), (0, 2 * WIDTH, 2 * WIDTH), (1, 0, 2 * WIDTH), (1, 2 * WIDTH, 2 * WIDTH))
 
 
@@ -67,14 +69,19 @@
     start_load(1)
 
     barrier = pltpu.get_barrier_semaphore()
-    lead = me == 0
-    beside = (twin, y_up, y_down, z_up, z_down)
+    lead = jnp.logical_and(core == 1, me == 0)
+    beside = (y_up, y_down, z_up, z_down)
 
     def greet(where, who):
         pl.semaphore_signal(barrier, inc=1, device_id=(where, who), device_id_type=MESH)
 
+    @pl.when(core == 0)
+    def _():
+        for peer in (across, right, left):
+            greet(bank, peer)
+
     for step in range(1, 4):
-        @pl.when(me + step < 4)
+        @pl.when(jnp.logical_and(core == 1, me + step < 4))
         def _():
             greet(bank, lax.rem(me + step, 4))
 
@@ -84,7 +91,7 @@
             greet(where, 0)
 
     for i in range(1, 4):
-        @pl.when(me == i)
+        @pl.when(jnp.logical_and(core == 1, me == i))
         def _():
             pl.semaphore_wait(barrier, i)
             for j in range(i):
@@ -125,8 +132,12 @@
     pltpu.make_async_copy(router_w, router_in.at[pl.ds(0, 1)], router_sem).start()
     pltpu.make_async_copy(router_g, router_in.at[pl.ds(1, 1)], router_sem).start()
 
+    @pl.when(core == 0)
+    def _():
+        pl.semaphore_wait(barrier, 3)
+
     for i in range(3):
-        @pl.when(me == i)
+        @pl.when(jnp.logical_and(core == 1, me == i))
         def _():
             pl.semaphore_wait(joined, 3 - i)
 
@@ -192,14 +203,20 @@
         normalised(c)
         send_both(where_at(c, me), late_recv, up_recv.at[0 if c < 2 * PER - 1 else 1])
 
+    @pl.when(jnp.logical_and(core == 0, me == 0))
+    def _():
+        greet(twin, 0)
+
     @pl.when(lead)
     def _():
         pl.semaphore_wait(barrier, 5)
         for where in beside:
             pl.semaphore_signal(ready, inc=1, device_id=(where, 0), device_id_type=MESH)
-        pl.semaphore_wait(ready, 5)
+        pl.semaphore_wait(ready, 4)
         for j in range(1, 4):
             pl.semaphore_signal(go, inc=1, device_id=(bank, j), device_id_type=MESH)
+        for j in range(4):
+            pl.semaphore_signal(go, inc=1, device_id=(twin, j), device_id_type=MESH)
 
     @pl.when(jnp.logical_not(lead))
     def _():
@@ -246,12 +263,16 @@
 
     short = RAW * HALF // COLS
     arrived(o_gate.at[pl.ds(0, ROWS - short)], gate_recv.at[0])
-    block = o_gate.at[pl.ds(left * ROWS, ROWS)]
-    remote(block, block, pass_send, pass_recv.at[0], bank, right).start()
-    for k, (first, count) in enumerate(((0, COLS - WIDTH), (COLS - WIDTH, WIDTH))):
-        block = o_up.at[pl.ds(right * ROWS, ROWS), pl.ds(first, count)]
-        arrived(block, up_recv.at[k])
-        remote(block, block, pass_send, pass_recv.at[1], bank, left).start()
+    for which, width in enumerate(FIRST):
+        @pl.when(core == which)
+        def _():
+            block = o_gate.at[pl.ds(left * ROWS, ROWS), pl.ds(0, width)]
+            remote(block, block, pass_send, pass_recv.at[0], bank, right).start()
+            for k, (first, end) in enumerate(((0, COLS - WIDTH), (COLS - WIDTH, COLS))):
+                arrived(o_up.at[pl.ds(0, ROWS), pl.ds(first, end - first)], up_recv.at[k])
+                if first < width:
+                    block = o_up.at[pl.ds(right * ROWS, ROWS), pl.ds(first, min(end, width) - first)]
+                    remote(block, block, pass_send, pass_recv.at[1], bank, left).start()
 
     arrived(o_gate.at[pl.ds(0, ROWS - short)], gate_recv.at[1])
     arrived(o_up.at[pl.ds(0, ROWS)], late_recv)
@@ -260,24 +281,89 @@
     departed(xr.at[pl.ds(0, 3)], x_send)
     departed(bank_r.at[pl.ds(0, 63)], b_send)
     departed(o_gate.at[pl.ds(0, 4 * ROWS - 2 * short)], bulk_send)
-    arrived(o_gate.at[pl.ds(0, ROWS)], pass_recv.at[0])
-    arrived(o_up.at[pl.ds(0, ROWS)], pass_recv.at[1])
-    departed(o_gate.at[pl.ds(0, 2 * ROWS)], pass_send)
-
-
-def put_out(gate, up, sgate, sup, router, o_gate, o_up, o_sgate, o_sup, o_router, sem):
+    for which, width in enumerate(FIRST):
+        @pl.when(core == which)
+        def _():
+            arrived(o_gate.at[pl.ds(0, ROWS), pl.ds(0, width)], pass_recv.at[0])
+            arrived(o_up.at[pl.ds(0, ROWS), pl.ds(0, width)], pass_recv.at[1])
+            departed(o_gate.at[pl.ds(0, 2 * ROWS), pl.ds(0, width)], pass_send)
+
+
+def put_first(gate, up, sgate, sup, router, o_gate, o_up, o_sgate, o_sup, o_router, done, sem):
+    me, core = lax.axis_index("zero"), lax.rem(lax.axis_index("bank"), 2)
+    pairs = ((gate, o_gate), (up, o_up))
+
+    def block(ref, step, width):
+        return ref.at[pl.ds(lax.rem(me + step, 4) * ROWS, ROWS), pl.ds(0, width)]
+
+    done[...] = jnp.zeros_like(done)
     copies = []
-    for i, (a, b) in enumerate(((gate, o_gate), (up, o_up))):
-        for k in range(4):
-            rows = pl.ds(k * ROWS, ROWS)
-            copies.append(pltpu.make_async_copy(a.at[rows], b.at[rows], sem.at[4 * i + k]))
+    for i, (a, b) in enumerate(pairs):
+        for k, step in enumerate((0, 1, 3)):
+            copies.append(pltpu.make_async_copy(block(a, step, COLS), block(b, step, COLS), sem.at[4 * i + k]))
     copies.append(pltpu.make_async_copy(router, o_router, sem.at[8]))
     copies.append(pltpu.make_async_copy(sgate, o_sgate, sem.at[9]))
     copies.append(pltpu.make_async_copy(sup, o_sup, sem.at[10]))
     for copy in copies:
         copy.start()
+    for which, width in enumerate(FIRST):
+        @pl.when(core == which)
+        def _():
+            far = [
+                pltpu.make_async_copy(block(a, 2, width), block(b, 2, width), sem.at[4 * i + 3])
+                for i, (a, b) in enumerate(pairs)
+            ]
+            for copy in far:
+                copy.start()
+            for copy in far:
+                copy.wait()
+
     for copy in copies:
         copy.wait()
+
+
+def pass_rest(gate, up, _, far_gate, far_up, send, recv):
+    bank = lax.axis_index("bank")
+    me = lax.axis_index("zero")
+    right, left = lax.rem(me + 1, 4), lax.rem(me + 3, 4)
+    barrier = pltpu.get_barrier_semaphore()
+    for peer in (right, left):
+        pl.semaphore_signal(barrier, inc=1, device_id=(bank, peer), device_id_type=MESH)
+    pl.semaphore_wait(barrier, 2)
+    for which, width in enumerate(FIRST):
+        @pl.when(lax.rem(bank, 2) == which)
+        def _():
+            copies = []
+            for k, (src, dst, owner, dest) in enumerate(((gate, far_gate, left, right), (up, far_up, right, left))):
+                copies.append(pltpu.make_async_remote_copy(
+                    src_ref=src.at[pl.ds(owner * ROWS, ROWS), pl.ds(width, COLS - width)],
+                    dst_ref=dst.at[:, pl.ds(0, COLS - width)],
+                    send_sem=send.at[k], recv_sem=recv.at[k],
+                    device_id=(bank, dest), device_id_type=MESH,
+                ))
+            for copy in copies:
+                copy.start()
+            for copy in copies:
+                copy.wait()
+
+
+def put_rest(far_gate, far_up, in_gate, in_up, o_gate, o_up, sem):
+    me, core = lax.axis_index("zero"), lax.rem(lax.axis_index("bank"), 2)
+    for which, width in enumerate(FIRST):
+        @pl.when(core == which)
+        def _():
+            copies = [
+                pltpu.make_async_copy(
+                    a.at[:, pl.ds(0, COLS - width)],
+                    b.at[pl.ds(lax.rem(me + 2, 4) * ROWS, ROWS), pl.ds(width, COLS - width)],
+                    sem.at[i],
+                )
+                for i, (a, b) in enumerate(((far_gate, o_gate), (far_up, o_up)))
+            ]
+            for copy in copies:
+                copy.start()
+            for copy in copies:
+                copy.wait()
 
 
 def local(w_gate, avg_gate, w_up, avg_up, mix_share, router_weight, router_gain):
@@ -334,15 +420,37 @@
         w_gate[0], avg_gate[0], w_up[0], avg_up[0], mix_share,
         router_weight.T, router_gain[None, :],
     )
-    gate, up, sgate, sup, router = pl.pallas_call(
-        put_out,
-        out_shape=tuple(jax.ShapeDtypeStruct(*r) for r in results),
+    results = tuple(jax.ShapeDtypeStruct(*r) for r in results)
+    gate, up, sgate, sup, router, done = pl.pallas_call(
+        put_first,
+        out_shape=results + (pltpu.VMEM((8, 128), f32),),
         in_specs=[in_vmem] * 5,
-        out_specs=[anywhere] * 5,
+        out_specs=[anywhere] * 5 + [in_vmem],
         scratch_shapes=[dma((11,))],
         compiler_params=pltpu.CompilerParams(vmem_limit_bytes=1024 * 1024),
-        name="put_out",
+        name="put_first",
     )(*held)
+    far = pl.pallas_call(
+        pass_rest,
+        out_shape=(pltpu.VMEM((ROWS, REST), bf16),) * 2,
+        in_specs=[in_vmem] * 3,
+        out_specs=[in_vmem] * 2,
+        scratch_shapes=[dma((2,)), dma((2,))],
+        compiler_params=pltpu.CompilerParams(
+            collective_id=1, has_side_effects=True, vmem_limit_bytes=1024 * 1024
+        ),
+        name="pass_rest",
+    )(held[0], held[1], done)
+    gate, up = pl.pallas_call(
+        put_rest,
+        out_shape=results[:2],
+        in_specs=[in_vmem] * 2 + [anywhere] * 2,
+        out_specs=[anywhere] * 2,
+        scratch_shapes=[dma((2,))],
+        input_output_aliases={2: 0, 3: 1},
+        compiler_params=pltpu.CompilerParams(vmem_limit_bytes=1024 * 1024),
+        name="put_rest",
+    )(*far, gate, up)
     return gate[None], up[None], sgate, sup, router.T
 
 

time: 80.5 us -> 77.5 us (0.963)
  Pallas kernels: 79.1 us -> 76.1 us
    pallas_call x1, Pallas kernels: 75.6 us -> 63.5 us  [local(): pl.pallas_call(kernel, out_shape=tuple((pltpu.VMEM(*r) for r in results))...]
    pallas_call x1 -> x3, Pallas kernels: 3.45 us -> 12.6 us  [the longest x1 8.43 us: local(): pl.pallas_call(pass_rest, out_shape=(pltpu.VMEM((ROWS, REST), bf16),) * 2...]
where the time goes in v5:
time: 77.5 us; the launch traced here: 77.4 us
  Pallas kernels  76.1 us (98%)
  between operations  1.3 us (2%)
    pallas_call x1, Pallas kernels, local(): pl.pallas_call(kernel, out_shape=tuple((pltpu.VMEM(*r) for r in results))...  63.5 us
    pallas_call x1, Pallas kernels, local(): pl.pallas_call(pass_rest, out_shape=(pltpu.VMEM((ROWS, REST), bf16),) * 2...  8.43 us
    pallas_call x1, Pallas kernels, local(): pl.pallas_call(put_first, out_shape=results + (pltpu.VMEM((8, 128), f32),...  3.34 us

profile of v5, /device:TPU:8, one launch (start us, length us, event | category | flops | bytes accessed | tf_op | source)
XLA Modules:
  0.0 77.4 jit_solution(10597976016655809438)
XLA Ops:
  1.3 63.5 %mean_and_gather.1 = (bf16[2048,1024]{1,0:T(8,128)(2,1)S(1)}, bf16[2048,1024]{1,0:T(8,128)(2,1)S(1)}, f32[1,1024]{1,0:T(1,128)S(1)}, f32[1,1024]{1,0:T(1,128)S(1)}, bf16[64,2048]{1,0:T(8,128)(2,1)S(1)}) custom-call(f32[512,1024]{1,0:T(8,128)} %bitcast.11, f32[512,1024]{1,0:T(8,128)} %bitcast.12, f32[512,1024]{1,0:T(8,128)} %bitcast.13, ...), custom_call_target="tpu_custom_call" | custom-call | tf_op jit(solution)/shard_map/mean_and_gather/pallas_call | solution.py:378
  64.8 3.3 %put_first.1 = (bf16[2048,1024]{1,0:T(8,128)(2,1)}, bf16[2048,1024]{1,0:T(8,128)(2,1)}, f32[1,1024]{1,0:T(1,128)}, f32[1,1024]{1,0:T(1,128)}, bf16[64,2048]{1,0:T(8,128)(2,1)}, /*index=5*/f32[8,128]{1,0:T(8,128)S(1)}) custom-call(bf16[2048,1024]{1,0:T(8,128)(2,1)S(1)} %get-tuple-element.20.gate, bf16[2048,1024]{1,0:T(8,128)(2,1)S(1)} %get-tuple-element.21.up, ...), custom_call_target="tpu_custom_call" | custom-call | tf_op jit(solution)/shard_map/put_first/pallas_call | solution.py:424
  68.2 8.4 %pass_rest.1 = (bf16[512,896]{1,0:T(8,128)(2,1)S(1)}, bf16[512,896]{1,0:T(8,128)(2,1)S(1)}) custom-call(bf16[2048,1024]{1,0:T(8,128)(2,1)S(1)} %get-tuple-element.20.gate, bf16[2048,1024]{1,0:T(8,128)(2,1)S(1)} %get-tuple-element.21.up, f32[8,128]{1,0:T(8,128)S(1)} %get-tuple-element.25._), custom_call_target="tpu_custom_call" | custom-call | tf_op jit(solution)/shard_map/pass_rest/pallas_call | solution.py:433
  76.6 0.8 %put_rest.1 = (bf16[2048,1024]{1,0:T(8,128)(2,1)}, bf16[2048,1024]{1,0:T(8,128)(2,1)}) custom-call(bf16[512,896]{1,0:T(8,128)(2,1)S(1)} %get-tuple-element.26.far_gate, bf16[512,896]{1,0:T(8,128)(2,1)S(1)} %get-tuple-element.27.far_up, bf16[2048,1024]{1,0:T(8,128)(2,1)} %get-tuple-element.28.in_gate, ...), custom_call_target="tpu_custom_call", output_to_operand_aliasing={{0}: (2, {}), {1}: (3, {})} | custom-call | tf_op jit(solution)/shard_map/put_rest/pallas_call | solution.py:444

commit v6 on v5

--- a/solution.py
+++ b/solution.py
@@ -13,6 +13,7 @@
 PER = COLS // WIDTH
 STEP = 128
 RB = 16
+SOON = 64
 RAW = 320
 FIRST = (768, 128)
 REST = COLS - min(FIRST)
@@ -25,7 +26,7 @@
     wide, other, load_sem, router_in, router_sem,
     sums0, sums1, sums2, sums_send, sums_recv, raw_in, raw_send, raw_recv,
     bulk_send, gate_recv, up_recv, late_recv, pass_send, pass_recv,
-    xr, bank_r, x_send, x_recv, b_send, twin_recv, y_recv, z_recv, joined, ready, go,
+    xr, bank_r, x_send, x_recv, b_send, twin_recv, y_recv, z_recv, joined, ready, go, opposite,
 ):
     bank = lax.axis_index("bank")
     me = lax.axis_index("zero")
@@ -77,7 +78,7 @@
 
     @pl.when(core == 0)
     def _():
-        for peer in (across, right, left):
+        for peer in (right, left):
             greet(bank, peer)
 
     for step in range(1, 4):
@@ -116,7 +117,7 @@
 
     peers = (across, right, left)
 
-    def share_sums(buf, k):
+    def share_sums(buf, k, peers=peers):
         for peer in peers:
             remote(buf.at[me], buf.at[me], sums_send, sums_recv.at[k], bank, peer).start()
 
@@ -134,28 +135,36 @@
 
     @pl.when(core == 0)
     def _():
-        pl.semaphore_wait(barrier, 3)
+        pl.semaphore_wait(barrier, 2)
+        pl.semaphore_signal(opposite, inc=1, device_id=(bank, right), device_id_type=MESH)
 
     for i in range(3):
         @pl.when(jnp.logical_and(core == 1, me == i))
         def _():
             pl.semaphore_wait(joined, 3 - i)
 
-    share_sums(sums0, 0)
-
-    def send_raw(k):
-        rows = pl.ds(k * RAW // 2, RAW // 2)
+    share_sums(sums0, 0, (right, left))
+
+    def send_raw(first, count):
+        rows = pl.ds(first, count)
         for side, dest in enumerate((right, left)):
             remote(wide.at[0, rows, pl.ds(0, HALF)], raw_in.at[side, rows], raw_send, raw_recv, bank, dest).start()
 
-    send_raw(0)
+    send_raw(0, SOON)
+
+    @pl.when(core == 0)
+    def _():
+        pl.semaphore_wait(opposite, 1)
+
+    share_sums(sums0, 0, (across,))
+    send_raw(SOON, RAW // 2 - SOON)
     loaded(1)
     sums1[me, :, pl.ds(0, WIDTH)] = mixed(1)
     loaded(2)
     for c in range(2, PER):
         sums1[me, :, pl.ds((c - 1) * WIDTH, WIDTH)] = mixed(c)
     share_sums(sums1, 1)
-    send_raw(1)
+    send_raw(RAW // 2, RAW // 2)
     for k in (3, 4):
         loaded(k)
         for c in (2 * k - 2, 2 * k - 1):
@@ -408,6 +417,7 @@
             dma(()),
             dma((2,)),
             dma((6,)),
+            regular,
             regular,
             regular,
             regular,

time: 77.5 us -> 77.4 us (level)
  no operation moved by 1% of the time
where the time goes in v6:
time: 77.4 us; the launch traced here: 77.3 us
  Pallas kernels  76 us (98%)
  between operations  1.3 us (2%)
    pallas_call x1, Pallas kernels, local(): pl.pallas_call(kernel, out_shape=tuple((pltpu.VMEM(*r) for r in results))...  64 us
    pallas_call x1, Pallas kernels, local(): pl.pallas_call(pass_rest, out_shape=(pltpu.VMEM((ROWS, REST), bf16),) * 2...  7.88 us
    pallas_call x1, Pallas kernels, local(): pl.pallas_call(put_first, out_shape=results + (pltpu.VMEM((8, 128), f32),...  3.34 us

profile of v6, /device:TPU:8, one launch (start us, length us, event | category | flops | bytes accessed | tf_op | source)
XLA Modules:
  0.0 77.3 jit_solution(2912544797775985374)
XLA Ops:
  1.3 64.0 %mean_and_gather.1 = (bf16[2048,1024]{1,0:T(8,128)(2,1)S(1)}, bf16[2048,1024]{1,0:T(8,128)(2,1)S(1)}, f32[1,1024]{1,0:T(1,128)S(1)}, f32[1,1024]{1,0:T(1,128)S(1)}, bf16[64,2048]{1,0:T(8,128)(2,1)S(1)}) custom-call(f32[512,1024]{1,0:T(8,128)} %bitcast.11, f32[512,1024]{1,0:T(8,128)} %bitcast.12, f32[512,1024]{1,0:T(8,128)} %bitcast.13, ...), custom_call_target="tpu_custom_call" | custom-call | tf_op jit(solution)/shard_map/mean_and_gather/pallas_call | solution.py:387
  65.2 3.3 %put_first.1 = (bf16[2048,1024]{1,0:T(8,128)(2,1)}, bf16[2048,1024]{1,0:T(8,128)(2,1)}, f32[1,1024]{1,0:T(1,128)}, f32[1,1024]{1,0:T(1,128)}, bf16[64,2048]{1,0:T(8,128)(2,1)}, /*index=5*/f32[8,128]{1,0:T(8,128)S(1)}) custom-call(bf16[2048,1024]{1,0:T(8,128)(2,1)S(1)} %get-tuple-element.20.gate, bf16[2048,1024]{1,0:T(8,128)(2,1)S(1)} %get-tuple-element.21.up, ...), custom_call_target="tpu_custom_call" | custom-call | tf_op jit(solution)/shard_map/put_first/pallas_call | solution.py:434
  68.6 7.9 %pass_rest.1 = (bf16[512,896]{1,0:T(8,128)(2,1)S(1)}, bf16[512,896]{1,0:T(8,128)(2,1)S(1)}) custom-call(bf16[2048,1024]{1,0:T(8,128)(2,1)S(1)} %get-tuple-element.20.gate, bf16[2048,1024]{1,0:T(8,128)(2,1)S(1)} %get-tuple-element.21.up, f32[8,128]{1,0:T(8,128)S(1)} %get-tuple-element.25._), custom_call_target="tpu_custom_call" | custom-call | tf_op jit(solution)/shard_map/pass_rest/pallas_call | solution.py:443
  76.5 0.8 %put_rest.1 = (bf16[2048,1024]{1,0:T(8,128)(2,1)}, bf16[2048,1024]{1,0:T(8,128)(2,1)}) custom-call(bf16[512,896]{1,0:T(8,128)(2,1)S(1)} %get-tuple-element.26.far_gate, bf16[512,896]{1,0:T(8,128)(2,1)S(1)} %get-tuple-element.27.far_up, bf16[2048,1024]{1,0:T(8,128)(2,1)} %get-tuple-element.28.in_gate, ...), custom_call_target="tpu_custom_call", output_to_operand_aliasing={{0}: (2, {}), {1}: (3, {})} | custom-call | tf_op jit(solution)/shard_map/put_rest/pallas_call | solution.py:454

commit v7 on v5

--- a/solution.py
+++ b/solution.py
@@ -14,7 +14,7 @@
 STEP = 128
 RB = 16
 RAW = 320
-FIRST = (768, 128)
+FIRST = (768, 0)
 REST = COLS - min(FIRST)
 LOADS = ((0, 0, WIDTH), (0, WIDTH, WIDTH), (0, 2 * WIDTH, 2 * WIDTH), (1, 0, 2 * WIDTH), (1, 2 * WIDTH, 2 * WIDTH))
 
@@ -55,18 +55,19 @@
     def departed(ref, sem):
         remote(ref, ref, sem, sem, bank, right).wait_send()
 
-    def start_load(k):
+    def start_load(k, pieces=1):
         m, first, count = LOADS[k]
         cols = pl.ds(first, count)
-        pltpu.make_async_copy(w_in[m].at[:, cols], wide.at[m, :, cols], load_sem.at[k]).start()
-        pltpu.make_async_copy(a_in[m].at[:, cols], other.at[m, :, cols], load_sem.at[k]).start()
+        for p in range(pieces):
+            rows = pl.ds(p * ROWS // pieces, ROWS // pieces)
+            pltpu.make_async_copy(w_in[m].at[rows, cols], wide.at[m, rows, cols], load_sem.at[k]).start()
+            pltpu.make_async_copy(a_in[m].at[rows, cols], other.at[m, rows, cols], load_sem.at[k]).start()
 
     def loaded(k):
         both = pl.ds(0, 2 * LOADS[k][2])
         pltpu.make_async_copy(w_gate.at[:, both], wide.at[0, :, both], load_sem.at[k]).wait()
 
-    start_load(0)
-    start_load(1)
+    start_load(0, 4)
 
     barrier = pltpu.get_barrier_semaphore()
     lead = jnp.logical_and(core == 1, me == 0)
@@ -125,10 +126,11 @@
         return jnp.sqrt(((buf[0] + buf[1]) + buf[2]) + buf[3])
 
     loaded(0)
-    sums0[me] = mixed(0)
+    start_load(1)
     start_load(2)
     start_load(3)
     start_load(4)
+    sums0[me] = mixed(0)
     pltpu.make_async_copy(router_w, router_in.at[pl.ds(0, 1)], router_sem).start()
     pltpu.make_async_copy(router_g, router_in.at[pl.ds(1, 1)], router_sem).start()
 
@@ -266,8 +268,9 @@
     for which, width in enumerate(FIRST):
         @pl.when(core == which)
         def _():
-            block = o_gate.at[pl.ds(left * ROWS, ROWS), pl.ds(0, width)]
-            remote(block, block, pass_send, pass_recv.at[0], bank, right).start()
+            if width:
+                block = o_gate.at[pl.ds(left * ROWS, ROWS), pl.ds(0, width)]
+                remote(block, block, pass_send, pass_recv.at[0], bank, right).start()
             for k, (first, end) in enumerate(((0, COLS - WIDTH), (COLS - WIDTH, COLS))):
                 arrived(o_up.at[pl.ds(0, ROWS), pl.ds(first, end - first)], up_recv.at[k])
                 if first < width:
@@ -282,6 +285,9 @@
     departed(bank_r.at[pl.ds(0, 63)], b_send)
     departed(o_gate.at[pl.ds(0, 4 * ROWS - 2 * short)], bulk_send)
     for which, width in enumerate(FIRST):
+        if not width:
+            continue
+
         @pl.when(core == which)
         def _():
             arrived(o_gate.at[pl.ds(0, ROWS), pl.ds(0, width)], pass_recv.at[0])
@@ -307,6 +313,9 @@
     for copy in copies:
         copy.start()
     for which, width in enumerate(FIRST):
+        if not width:
+            continue
+
         @pl.when(core == which)
         def _():
             far = [

time: 77.5 us -> 77.5 us (level)
  no operation moved by 1% of the time
where the time goes in v7:
time: 77.5 us; the launch traced here: 77.4 us
  Pallas kernels  76.1 us (98%)
  between operations  1.3 us (2%)
    pallas_call x1, Pallas kernels, local(): pl.pallas_call(kernel, out_shape=tuple((pltpu.VMEM(*r) for r in results))...  63.6 us
    pallas_call x1, Pallas kernels, local(): pl.pallas_call(pass_rest, out_shape=(pltpu.VMEM((ROWS, REST), bf16),) * 2...  8.34 us
    pallas_call x1, Pallas kernels, local(): pl.pallas_call(put_first, out_shape=results + (pltpu.VMEM((8, 128), f32),...  3.34 us

profile of v7, /device:TPU:8, one launch (start us, length us, event | category | flops | bytes accessed | tf_op | source)
XLA Modules:
  0.0 77.4 jit_solution(13711750645836879710)
XLA Ops:
  1.3 63.6 %mean_and_gather.1 = (bf16[2048,1024]{1,0:T(8,128)(2,1)S(1)}, bf16[2048,1024]{1,0:T(8,128)(2,1)S(1)}, f32[1,1024]{1,0:T(1,128)S(1)}, f32[1,1024]{1,0:T(1,128)S(1)}, bf16[64,2048]{1,0:T(8,128)(2,1)S(1)}) custom-call(f32[512,1024]{1,0:T(8,128)} %bitcast.11, f32[512,1024]{1,0:T(8,128)} %bitcast.12, f32[512,1024]{1,0:T(8,128)} %bitcast.13, ...), custom_call_target="tpu_custom_call" | custom-call | tf_op jit(solution)/shard_map/mean_and_gather/pallas_call | solution.py:387
  64.9 3.3 %put_first.1 = (bf16[2048,1024]{1,0:T(8,128)(2,1)}, bf16[2048,1024]{1,0:T(8,128)(2,1)}, f32[1,1024]{1,0:T(1,128)}, f32[1,1024]{1,0:T(1,128)}, bf16[64,2048]{1,0:T(8,128)(2,1)}, /*index=5*/f32[8,128]{1,0:T(8,128)S(1)}) custom-call(bf16[2048,1024]{1,0:T(8,128)(2,1)S(1)} %get-tuple-element.20.gate, bf16[2048,1024]{1,0:T(8,128)(2,1)S(1)} %get-tuple-element.21.up, ...), custom_call_target="tpu_custom_call" | custom-call | tf_op jit(solution)/shard_map/put_first/pallas_call | solution.py:433
  68.2 8.3 %pass_rest.1 = (bf16[512,1024]{1,0:T(8,128)(2,1)S(1)}, bf16[512,1024]{1,0:T(8,128)(2,1)S(1)}) custom-call(bf16[2048,1024]{1,0:T(8,128)(2,1)S(1)} %get-tuple-element.20.gate, bf16[2048,1024]{1,0:T(8,128)(2,1)S(1)} %get-tuple-element.21.up, f32[8,128]{1,0:T(8,128)S(1)} %get-tuple-element.25._), custom_call_target="tpu_custom_call" | custom-call | tf_op jit(solution)/shard_map/pass_rest/pallas_call | solution.py:442
  76.6 0.8 %put_rest.1 = (bf16[2048,1024]{1,0:T(8,128)(2,1)}, bf16[2048,1024]{1,0:T(8,128)(2,1)}) custom-call(bf16[512,1024]{1,0:T(8,128)(2,1)S(1)} %get-tuple-element.26.far_gate, bf16[512,1024]{1,0:T(8,128)(2,1)S(1)} %get-tuple-element.27.far_up, bf16[2048,1024]{1,0:T(8,128)(2,1)} %get-tuple-element.28.in_gate, ...), custom_call_target="tpu_custom_call", output_to_operand_aliasing={{0}: (2, {}), {1}: (3, {})} | custom-call | tf_op jit(solution)/shard_map/put_rest/pallas_call | solution.py:453

commit v8 on v7

--- a/solution.py
+++ b/solution.py
@@ -67,7 +67,6 @@
         both = pl.ds(0, 2 * LOADS[k][2])
         pltpu.make_async_copy(w_gate.at[:, both], wide.at[0, :, both], load_sem.at[k]).wait()
 
-    start_load(0, 4)
 
     barrier = pltpu.get_barrier_semaphore()
     lead = jnp.logical_and(core == 1, me == 0)
@@ -90,6 +89,8 @@
     def _():
         for where in beside:
             greet(where, 0)
+
+    start_load(0, 4)
 
     for i in range(1, 4):
         @pl.when(jnp.logical_and(core == 1, me == i))

time: 77.5 us -> 77.5 us (level)
  no operation moved by 1% of the time
where the time goes in v8:
time: 77.5 us; the launch traced here: 77.4 us
  Pallas kernels  76.1 us (98%)
  between operations  1.3 us (2%)
    pallas_call x1, Pallas kernels, local(): pl.pallas_call(kernel, out_shape=tuple((pltpu.VMEM(*r) for r in results))...  63.6 us
    pallas_call x1, Pallas kernels, local(): pl.pallas_call(pass_rest, out_shape=(pltpu.VMEM((ROWS, REST), bf16),) * 2...  8.33 us
    pallas_call x1, Pallas kernels, local(): pl.pallas_call(put_first, out_shape=results + (pltpu.VMEM((8, 128), f32),...  3.34 us

profile of v8, /device:TPU:8, one launch (start us, length us, event | category | flops | bytes accessed | tf_op | source)
XLA Modules:
  0.0 77.4 jit_solution(2755939676890357051)
XLA Ops:
  1.3 63.6 %mean_and_gather.1 = (bf16[2048,1024]{1,0:T(8,128)(2,1)S(1)}, bf16[2048,1024]{1,0:T(8,128)(2,1)S(1)}, f32[1,1024]{1,0:T(1,128)S(1)}, f32[1,1024]{1,0:T(1,128)S(1)}, bf16[64,2048]{1,0:T(8,128)(2,1)S(1)}) custom-call(f32[512,1024]{1,0:T(8,128)} %bitcast.11, f32[512,1024]{1,0:T(8,128)} %bitcast.12, f32[512,1024]{1,0:T(8,128)} %bitcast.13, ...), custom_call_target="tpu_custom_call" | custom-call | tf_op jit(solution)/shard_map/mean_and_gather/pallas_call | solution.py:388
  64.9 3.3 %put_first.1 = (bf16[2048,1024]{1,0:T(8,128)(2,1)}, bf16[2048,1024]{1,0:T(8,128)(2,1)}, f32[1,1024]{1,0:T(1,128)}, f32[1,1024]{1,0:T(1,128)}, bf16[64,2048]{1,0:T(8,128)(2,1)}, /*index=5*/f32[8,128]{1,0:T(8,128)S(1)}) custom-call(bf16[2048,1024]{1,0:T(8,128)(2,1)S(1)} %get-tuple-element.20.gate, bf16[2048,1024]{1,0:T(8,128)(2,1)S(1)} %get-tuple-element.21.up, ...), custom_call_target="tpu_custom_call" | custom-call | tf_op jit(solution)/shard_map/put_first/pallas_call | solution.py:434
  68.2 8.3 %pass_rest.1 = (bf16[512,1024]{1,0:T(8,128)(2,1)S(1)}, bf16[512,1024]{1,0:T(8,128)(2,1)S(1)}) custom-call(bf16[2048,1024]{1,0:T(8,128)(2,1)S(1)} %get-tuple-element.20.gate, bf16[2048,1024]{1,0:T(8,128)(2,1)S(1)} %get-tuple-element.21.up, f32[8,128]{1,0:T(8,128)S(1)} %get-tuple-element.25._), custom_call_target="tpu_custom_call" | custom-call | tf_op jit(solution)/shard_map/pass_rest/pallas_call | solution.py:443
  76.6 0.8 %put_rest.1 = (bf16[2048,1024]{1,0:T(8,128)(2,1)}, bf16[2048,1024]{1,0:T(8,128)(2,1)}) custom-call(bf16[512,1024]{1,0:T(8,128)(2,1)S(1)} %get-tuple-element.26.far_gate, bf16[512,1024]{1,0:T(8,128)(2,1)S(1)} %get-tuple-element.27.far_up, bf16[2048,1024]{1,0:T(8,128)(2,1)} %get-tuple-element.28.in_gate, ...), custom_call_target="tpu_custom_call", output_to_operand_aliasing={{0}: (2, {}), {1}: (3, {})} | custom-call | tf_op jit(solution)/shard_map/put_rest/pallas_call | solution.py:454
